TPU v7x, 8 devices: a whole 2x2x1 slice. The times are simulated.
8 devices in a mesh: dp: 2 (over z, y), pp: 4 (over x, core).
Axes of the slice: x: 2, y: 2, z: 1, core: 2. Of those that a mesh axis runs over, the one named last changes fastest.
Arguments:
- inputs: bfloat16 [512, 32, 1000], P('dp'), parts along dimension 0
- targets: bfloat16 [512, 32, 1000], P('dp'), parts along dimension 0
- w_in: bfloat16 [4, 4, 1000, 4000], P('dp', 'pp'), parts along dimension 0
- w_hid: bfloat16 [4, 4, 1000, 4000], P('dp', 'pp'), parts along dimension 0
- bias: float32 [4, 4, 4000], P('dp', 'pp'), parts along dimension 0
- h_init: float32 [4, 4, 256, 1000], P('dp', 'pp'), parts along dimension 0
- c_init: float32 [4, 4, 256, 1000], P('dp', 'pp'), parts along dimension 0
Outputs:
- output 1: float32 [2], P('dp'), parts along dimension 0
- output 2: float32 [4, 4, 1000, 4000], P('dp', 'pp'), parts along dimension 0
- output 3: float32 [4, 4, 1000, 4000], P('dp', 'pp'), parts along dimension 0
- output 4: float32 [4, 4, 4000], P('dp', 'pp'), parts along dimension 0
- output 5: float32 [4, 4, 256, 1000], P('dp', 'pp'), parts along dimension 0
- output 6: float32 [4, 4, 256, 1000], P('dp', 'pp'), parts along dimension 0
There are 2 independent parts. A program takes and returns all parts, laid end to end along the dimension named above; each array names one.
All inputs are finite; a program needn't handle non-finite values.
Results may differ from a plain program's by a relative error of at most 0.00973023.
Values are sent between devices in bfloat16 or wider.
A program may use at most 1 GiB of HBM per device.

v0:
```python
import jax
import jax.numpy as jnp
from jax import lax
from jax.sharding import PartitionSpec as P

SPAN_STEPS = 8


def cell_step(proj_t, h_prev, c_prev, w_hid, bias_row):
    n_hidden = c_prev.shape[-1]
    pre_act = proj_t + jnp.dot(h_prev, w_hid, preferred_element_type=jnp.float32) + bias_row
    gate_i = jax.nn.sigmoid(pre_act[:, :n_hidden])
    gate_f = jax.nn.sigmoid(pre_act[:, n_hidden:2 * n_hidden])
    gate_g = jnp.tanh(pre_act[:, 2 * n_hidden:3 * n_hidden])
    gate_o = jax.nn.sigmoid(pre_act[:, 3 * n_hidden:])
    c_new = gate_f * c_prev + gate_i * gate_g
    h_new = (gate_o * jnp.tanh(c_new)).astype(jnp.bfloat16)
    return pre_act, c_new, h_new


def cell_grad(pre_act, c_prev, c_now, dh_total, dc_carry):
    n_hidden = c_now.shape[-1]
    gate_i = jax.nn.sigmoid(pre_act[:, :n_hidden])
    gate_f = jax.nn.sigmoid(pre_act[:, n_hidden:2 * n_hidden])
    gate_g = jnp.tanh(pre_act[:, 2 * n_hidden:3 * n_hidden])
    gate_o = jax.nn.sigmoid(pre_act[:, 3 * n_hidden:])
    tanh_c = jnp.tanh(c_now)
    dc_total = dc_carry + dh_total * gate_o * (1.0 - tanh_c * tanh_c)
    grad_pre = jnp.concatenate([dc_total * gate_g * gate_i * (1.0 - gate_i), dc_total * c_prev * gate_f * (1.0 - gate_f), dc_total * gate_i * (1.0 - gate_g * gate_g), dh_total * tanh_c * gate_o * (1.0 - gate_o)], axis=-1)
    return grad_pre, dc_total * gate_f


def seq_forward(seq_in, w_in, w_hid, bias_row, h_prev, c_prev):
    projected = jnp.einsum('tbh,hg->tbg', seq_in, w_in, preferred_element_type=jnp.float32)

    def step_fn(carry, proj_t):
        h_last, c_last = carry
        pre_act, c_new, h_new = cell_step(proj_t, h_last, c_last, w_hid, bias_row)
        return (h_new, c_new), (pre_act, c_new, h_new)

    (h_end, c_end), (pre_seq, cell_seq, h_seq) = lax.scan(step_fn, (h_prev, c_prev), projected)
    out_seq = (seq_in.astype(jnp.float32) + h_seq.astype(jnp.float32)).astype(jnp.bfloat16)
    return h_end, c_end, pre_seq, cell_seq, h_seq, out_seq


def seq_backward(seq_in, h_before, c_before, pre_seq, cell_seq, h_seq, grad_seq, w_in, w_hid, dh_carry, dc_carry):
    c_prevs = jnp.concatenate([c_before[None], cell_seq[:-1]], axis=0)
    h_prevs = jnp.concatenate([h_before[None], h_seq[:-1]], axis=0)

    def step_fn(carry, xs_t):
        dh_last, dc_last, bias_acc = carry
        pre_t, c_prev_t, c_now_t, grad_t = xs_t
        grad_pre, dc_new = cell_grad(pre_t, c_prev_t, c_now_t, grad_t + dh_last, dc_last)
        grad_low = grad_pre.astype(jnp.bfloat16)
        dh_new = jnp.einsum('bg,hg->bh', grad_low, w_hid, preferred_element_type=jnp.float32)
        return (dh_new, dc_new, bias_acc + jnp.sum(grad_pre, axis=0)), grad_low

    bias_zero = jnp.zeros((pre_seq.shape[-1],), jnp.float32)
    (dh_end, dc_end, grad_bias), grad_low_seq = lax.scan(step_fn, (dh_carry, dc_carry, bias_zero), (pre_seq, c_prevs, cell_seq, grad_seq), reverse=True)
    grad_wx = jnp.einsum('tbh,tbg->hg', seq_in, grad_low_seq, preferred_element_type=jnp.float32)
    grad_wh = jnp.einsum('tbh,tbg->hg', h_prevs, grad_low_seq, preferred_element_type=jnp.float32)
    grad_in = (grad_seq + jnp.einsum('tbg,hg->tbh', grad_low_seq, w_in, preferred_element_type=jnp.float32)).astype(jnp.bfloat16)
    return dh_end, dc_end, grad_wx, grad_wh, grad_bias, grad_in


def solution(mesh):
    n_stages = mesh.shape['pp']
    fwd_perm = [(sender, (sender + 1) % n_stages) for sender in range(n_stages)]
    bwd_perm = [(sender, (sender - 1) % n_stages) for sender in range(n_stages)]

    def local_fn(inputs, targets, w_in, w_hid, bias, h_init, c_init):
        n_batch, n_steps, n_hidden = inputs.shape
        n_pieces = n_steps // SPAN_STEPS
        n_ticks = n_pieces + 2 * n_stages - 1
        stage = lax.axis_index('pp')
        is_first = stage == 0
        is_last = stage == n_stages - 1
        w_in_loc = w_in[:, 0]
        w_hid_loc = w_hid[:, 0]
        bias_loc = bias[:, 0]
        h_start = h_init[:, 0].astype(jnp.bfloat16)
        c_start = c_init[:, 0]
        inputs_tm = jnp.swapaxes(inputs, 0, 1)
        full_shape = (n_steps, n_batch, n_hidden)
        inbox_init = jnp.zeros((2, SPAN_STEPS, n_batch, n_hidden), jnp.bfloat16)

        def window_of(buf, start):
            return lax.dynamic_slice_in_dim(buf, start, SPAN_STEPS, 0)

        def place(buf, piece, start):
            return lax.dynamic_update_slice_in_dim(buf, piece, start, 0)

        def round_state(k_round):
            state = (h_start[k_round], c_start[k_round], jnp.zeros((n_steps, n_batch, 4 * n_hidden), jnp.float32), jnp.zeros(full_shape, jnp.float32), jnp.zeros(full_shape, jnp.bfloat16), jnp.zeros(full_shape, jnp.bfloat16))
            if k_round == 1:
                state = state + (jnp.zeros(full_shape, jnp.bfloat16),)
            return state

        def fwd_tick(tick_idx, carry):
            inbox, rounds = carry
            new_rounds = []
            outbox = []
            for k_round in range(2):
                piece_idx = tick_idx - k_round * n_stages - stage
                active = (piece_idx >= 0) & (piece_idx < n_pieces)
                start = jnp.clip(piece_idx, 0, n_pieces - 1) * SPAN_STEPS
                if k_round == 0:
                    seq_piece = jnp.where(is_first, window_of(inputs_tm, start), inbox[0])
                else:
                    seq_piece = jnp.where(is_first, inbox[0], inbox[1])

                def run_piece(state, k_round=k_round, seq_piece=seq_piece, start=start):
                    h_end, c_end, pre_seq, cell_seq, h_seq, out_seq = seq_forward(seq_piece, w_in_loc[k_round], w_hid_loc[k_round], bias_loc[k_round], state[0], state[1])
                    stored = (h_end, c_end, place(state[2], pre_seq, start), place(state[3], cell_seq, start), place(state[4], h_seq, start), place(state[5], seq_piece, start))
                    if k_round == 1:
                        stored = stored + (place(state[6], out_seq, start),)
                    return stored, out_seq

                def skip_piece(state, seq_piece=seq_piece):
                    return state, seq_piece

                state_new, out_seq = lax.cond(active, run_piece, skip_piece, rounds[k_round])
                new_rounds.append(state_new)
                outbox.append(out_seq)
            inbox = lax.ppermute(jnp.stack(outbox), 'pp', fwd_perm)
            return inbox, tuple(new_rounds)

        _, fwd_rounds = lax.fori_loop(0, n_ticks, fwd_tick, (inbox_init, (round_state(0), round_state(1))))
        top_seq = fwd_rounds[1][6]
        inv_count = 1.0 / (n_batch * n_steps)
        error_seq = top_seq.astype(jnp.float32) - jnp.swapaxes(targets, 0, 1).astype(jnp.float32)
        local_loss = jnp.where(is_last, 0.5 * inv_count * jnp.sum(error_seq * error_seq), 0.0)
        loss = lax.psum(local_loss, 'pp')
        grad_top = error_seq * inv_count

        def bwd_tick(tick_idx, carry):
            inbox, accs = carry
            new_accs = []
            outbox = []
            for k_round in range(2):
                piece_rev = tick_idx - (1 - k_round) * n_stages - (n_stages - 1 - stage)
                active = (piece_rev >= 0) & (piece_rev < n_pieces)
                start = (n_pieces - 1 - jnp.clip(piece_rev, 0, n_pieces - 1)) * SPAN_STEPS
                if k_round == 1:
                    grad_piece = jnp.where(is_last, window_of(grad_top, start), inbox[1].astype(jnp.float32))
                else:
                    grad_piece = jnp.where(is_last, inbox[1], inbox[0]).astype(jnp.float32)

                def run_piece(state, k_round=k_round, grad_piece=grad_piece, start=start):
                    saved = fwd_rounds[k_round]
                    prev_idx = jnp.maximum(start - 1, 0)
                    has_prev = start > 0
                    c_before = jnp.where(has_prev, lax.dynamic_index_in_dim(saved[3], prev_idx, 0, keepdims=False), c_start[k_round])
                    h_before = jnp.where(has_prev, lax.dynamic_index_in_dim(saved[4], prev_idx, 0, keepdims=False), h_start[k_round])
                    dh_end, dc_end, grad_wx, grad_wh, grad_b, grad_in = seq_backward(window_of(saved[5], start), h_before, c_before, window_of(saved[2], start), window_of(saved[3], start), window_of(saved[4], start), grad_piece, w_in_loc[k_round], w_hid_loc[k_round], state[0], state[1])
                    return (dh_end, dc_end, state[2] + grad_wx, state[3] + grad_wh, state[4] + grad_b), grad_in

                def skip_piece(state, grad_piece=grad_piece):
                    return state, grad_piece.astype(jnp.bfloat16)

                state_new, grad_out = lax.cond(active, run_piece, skip_piece, accs[k_round])
                new_accs.append(state_new)
                outbox.append(grad_out)
            inbox = lax.ppermute(jnp.stack(outbox), 'pp', bwd_perm)
            return inbox, tuple(new_accs)

        zeros_state = jnp.zeros((n_batch, n_hidden), jnp.float32)
        zeros_weight = jnp.zeros((n_hidden, 4 * n_hidden), jnp.float32)
        acc_init = (zeros_state, zeros_state, zeros_weight, zeros_weight, jnp.zeros((4 * n_hidden,), jnp.float32))
        _, accs = lax.fori_loop(0, n_ticks, bwd_tick, (inbox_init, (acc_init, acc_init)))
        grad_h_init = jnp.stack([accs[0][0], accs[1][0]])[:, None]
        grad_c_init = jnp.stack([accs[0][1], accs[1][1]])[:, None]
        grad_w_in = jnp.stack([accs[0][2], accs[1][2]])[:, None]
        grad_w_hid = jnp.stack([accs[0][3], accs[1][3]])[:, None]
        grad_bias = jnp.stack([accs[0][4], accs[1][4]])[:, None]
        return loss[None], grad_w_in, grad_w_hid, grad_bias, grad_h_init, grad_c_init

    spec_seq = P('dp', None, None)
    spec_weight = P('dp', 'pp', None, None)
    spec_bias = P('dp', 'pp', None)
    return jax.shard_map(local_fn, mesh=mesh, in_specs=(spec_seq, spec_seq, spec_weight, spec_weight, spec_bias, spec_weight, spec_weight), out_specs=(P('dp'), spec_weight, spec_weight, spec_bias, spec_weight, spec_weight), check_vma=False)
```

profile of v0, /device:TPU:0, one launch (start us, length us, event | category | flops | bytes accessed | tf_op | source)
XLA Modules:
  0.0 7892.2 jit_solution(15796771136395665644)
XLA Ops:
  160.8 3179.5 %while.154 = (s32[]{:T(128)}, bf16[2,8,256,1000]{2,3,1,0:T(8,128)(2,1)}, bf16[256,1000]{0,1:T(8,128)(2,1)}, f32[256,1000]{0,1:T(8,128)}, f32[32,256,4000]{1,2,0:...) while((s32[]{:T(128)}, ...), condition=%wide.region_9.10_spmd, body=%wide.region_0.9_spmd.sunk | while | flops 36908032000 | bytes 588132736 | solution.py:128
  190.3 177.3 %conditional.9 = (bf16[256,1000]{0,1:T(8,128)(2,1)S(1)}, f32[256,1000]{0,1:T(8,128)S(1)}, f32[32,256,4000]{1,2,0:T(8,128)}, f32[32,256,1000]{1,2,0:T(8,128)}, bf...) conditional(s32[]{:T(128)} %convert_element_type.235, ...), branch_computations={%region_1.1_spmd, %region_2.4_spmd} | conditional | flops 18445824000 | bytes 251057920 | solution.py:122
  475.4 177.3 %conditional.9 = (bf16[256,1000]{0,1:T(8,128)(2,1)S(1)}, f32[256,1000]{0,1:T(8,128)S(1)}, f32[32,256,4000]{1,2,0:T(8,128)}, f32[32,256,1000]{1,2,0:T(8,128)}, bf...) conditional(s32[]{:T(128)} %convert_element_type.235, ...), branch_computations={%region_1.1_spmd, %region_2.4_spmd} | conditional | flops 18445824000 | bytes 251057920 | solution.py:122
  760.7 177.5 %conditional.9 = (bf16[256,1000]{0,1:T(8,128)(2,1)S(1)}, f32[256,1000]{0,1:T(8,128)S(1)}, f32[32,256,4000]{1,2,0:T(8,128)}, f32[32,256,1000]{1,2,0:T(8,128)}, bf...) conditional(s32[]{:T(128)} %convert_element_type.235, ...), branch_computations={%region_1.1_spmd, %region_2.4_spmd} | conditional | flops 18445824000 | bytes 251057920 | solution.py:122
  1046.0 177.5 %conditional.9 = (bf16[256,1000]{0,1:T(8,128)(2,1)S(1)}, f32[256,1000]{0,1:T(8,128)S(1)}, f32[32,256,4000]{1,2,0:T(8,128)}, f32[32,256,1000]{1,2,0:T(8,128)}, bf...) conditional(s32[]{:T(128)} %convert_element_type.235, ...), branch_computations={%region_1.1_spmd, %region_2.4_spmd} | conditional | flops 18445824000 | bytes 251057920 | solution.py:122
  1331.4 180.9 %conditional.8 = (bf16[256,1000]{0,1:T(8,128)(2,1)S(1)}, f32[256,1000]{0,1:T(8,128)S(1)}, f32[32,256,4000]{1,2,0:T(8,128)}, f32[32,256,1000]{1,2,0:T(8,128)}, bf...) conditional(s32[]{:T(128)} %convert_element_type.234, ...), branch_computations={%region_5.5_spmd, %region_6.8_spmd} | conditional | flops 18454016000 | bytes 255153952 | solution.py:122
  1620.2 180.7 %conditional.8 = (bf16[256,1000]{0,1:T(8,128)(2,1)S(1)}, f32[256,1000]{0,1:T(8,128)S(1)}, f32[32,256,4000]{1,2,0:T(8,128)}, f32[32,256,1000]{1,2,0:T(8,128)}, bf...) conditional(s32[]{:T(128)} %convert_element_type.234, ...), branch_computations={%region_5.5_spmd, %region_6.8_spmd} | conditional | flops 18454016000 | bytes 255153952 | solution.py:122
  1908.8 180.6 %conditional.8 = (bf16[256,1000]{0,1:T(8,128)(2,1)S(1)}, f32[256,1000]{0,1:T(8,128)S(1)}, f32[32,256,4000]{1,2,0:T(8,128)}, f32[32,256,1000]{1,2,0:T(8,128)}, bf...) conditional(s32[]{:T(128)} %convert_element_type.234, ...), branch_computations={%region_5.5_spmd, %region_6.8_spmd} | conditional | flops 18454016000 | bytes 255153952 | solution.py:122
  2197.3 180.8 %conditional.8 = (bf16[256,1000]{0,1:T(8,128)(2,1)S(1)}, f32[256,1000]{0,1:T(8,128)S(1)}, f32[32,256,4000]{1,2,0:T(8,128)}, f32[32,256,1000]{1,2,0:T(8,128)}, bf...) conditional(s32[]{:T(128)} %convert_element_type.234, ...), branch_computations={%region_5.5_spmd, %region_6.8_spmd} | conditional | flops 18454016000 | bytes 255153952 | solution.py:122
  2596.9 166.1 %collective-permute-done.1 = bf16[2,8,256,1000]{2,3,1,0:T(8,128)(2,1)} collective-permute-done((bf16[2,8,256,1000]{2,3,1,0:T(8,128)(2,1)}, bf16[2,8,256,1000]{2,3,1,0:T(8,128)(2,1)}, u32[]{:S(2)}, u32[]{:S(2)}) %collective-permute-start.1) | collective-permute-done | bytes 8192032 | tf_op jit(solution)/shard_map/while/body/eval_jaxpr/ppermute | solution.py:125
  2780.1 268.9 %collective-permute-done.1 = bf16[2,8,256,1000]{2,3,1,0:T(8,128)(2,1)} collective-permute-done((bf16[2,8,256,1000]{2,3,1,0:T(8,128)(2,1)}, bf16[2,8,256,1000]{2,3,1,0:T(8,128)(2,1)}, u32[]{:S(2)}, u32[]{:S(2)}) %collective-permute-start.1) | collective-permute-done | bytes 8192032 | tf_op jit(solution)/shard_map/while/body/eval_jaxpr/ppermute | solution.py:125
  3066.1 269.1 %collective-permute-done.1 = bf16[2,8,256,1000]{2,3,1,0:T(8,128)(2,1)} collective-permute-done((bf16[2,8,256,1000]{2,3,1,0:T(8,128)(2,1)}, bf16[2,8,256,1000]{2,3,1,0:T(8,128)(2,1)}, u32[]{:S(2)}, u32[]{:S(2)}) %collective-permute-start.1) | collective-permute-done | bytes 8192032 | tf_op jit(solution)/shard_map/while/body/eval_jaxpr/ppermute | solution.py:125
  3407.3 4428.0 %while.155 = (s32[]{:T(128)}, bf16[2,8,256,1000]{2,3,1,0:T(8,128)(2,1)}, f32[256,1000]{0,1:T(8,128)}, f32[256,1000]{0,1:T(8,128)}, f32[1000,4000]{1,0:T(8,128)},...) while((s32[]{:T(128)}, ...), condition=%wide.region_23.24_spmd, body=%wide.region_12.23_spmd.sunk | while | flops 102506635264 | bytes 825441920 | solution.py:170
  3452.2 261.7 %collective-permute-start = (bf16[2,8,256,1000]{2,3,1,0:T(8,128)(2,1)}, bf16[2,8,256,1000]{2,3,1,0:T(8,128)(2,1)}, u32[]{:S(2)}, u32[]{:S(2)}) collective-permute-start(bf16[2,8,256,1000]{2,3,1,0:T(8,128)(2,1)} %pad_maximum_fusion.10), channel_id=1, source_target_pairs={{0,3},{1,0},{2,1},{3,2},{4,7},{5,4},{6,5},{7,6}} | collective-permute-start | bytes 24576008 | tf_op jit(solution)/shard_map/while/body/eval_jaxpr/ppermute | solution.py:164
  3848.0 264.3 %collective-permute-start = (bf16[2,8,256,1000]{2,3,1,0:T(8,128)(2,1)}, bf16[2,8,256,1000]{2,3,1,0:T(8,128)(2,1)}, u32[]{:S(2)}, u32[]{:S(2)}) collective-permute-start(bf16[2,8,256,1000]{2,3,1,0:T(8,128)(2,1)} %pad_maximum_fusion.10), channel_id=1, source_target_pairs={{0,3},{1,0},{2,1},{3,2},{4,7},{5,4},{6,5},{7,6}} | collective-permute-start | bytes 24576008 | tf_op jit(solution)/shard_map/while/body/eval_jaxpr/ppermute | solution.py:164
  4246.0 264.4 %collective-permute-start = (bf16[2,8,256,1000]{2,3,1,0:T(8,128)(2,1)}, bf16[2,8,256,1000]{2,3,1,0:T(8,128)(2,1)}, u32[]{:S(2)}, u32[]{:S(2)}) collective-permute-start(bf16[2,8,256,1000]{2,3,1,0:T(8,128)(2,1)} %pad_maximum_fusion.10), channel_id=1, source_target_pairs={{0,3},{1,0},{2,1},{3,2},{4,7},{5,4},{6,5},{7,6}} | collective-permute-start | bytes 24576008 | tf_op jit(solution)/shard_map/while/body/eval_jaxpr/ppermute | solution.py:164
  4615.3 276.7 %conditional.10 = (f32[256,1000]{0,1:T(8,128)}, f32[256,1000]{0,1:T(8,128)}, f32[1000,4000]{1,0:T(8,128)}, f32[1000,4000]{1,0:T(8,128)}, f32[4000]{0:T(1024)}, /*index=5*/bf16[1,8,256,1000]{2,3,1,0:T(8,128)(2,1)}) conditional(s32[]{:T(128)} %convert_element_type.236, (f32[256,1000]{0,1:T(8,128)}, f32[256,1000]{0,1:T(8,128)}, ...), branch_computations={%region_18.18_spmd, %region_19.22_spmd} | conditional | flops 51247173632 | bytes 353328512 | solution.py:161
  5013.6 276.5 %conditional.10 = (f32[256,1000]{0,1:T(8,128)}, f32[256,1000]{0,1:T(8,128)}, f32[1000,4000]{1,0:T(8,128)}, f32[1000,4000]{1,0:T(8,128)}, f32[4000]{0:T(1024)}, /*index=5*/bf16[1,8,256,1000]{2,3,1,0:T(8,128)(2,1)}) conditional(s32[]{:T(128)} %convert_element_type.236, (f32[256,1000]{0,1:T(8,128)}, f32[256,1000]{0,1:T(8,128)}, ...), branch_computations={%region_18.18_spmd, %region_19.22_spmd} | conditional | flops 51247173632 | bytes 353328512 | solution.py:161
  5419.6 276.7 %conditional.10 = (f32[256,1000]{0,1:T(8,128)}, f32[256,1000]{0,1:T(8,128)}, f32[1000,4000]{1,0:T(8,128)}, f32[1000,4000]{1,0:T(8,128)}, f32[4000]{0:T(1024)}, /*index=5*/bf16[1,8,256,1000]{2,3,1,0:T(8,128)(2,1)}) conditional(s32[]{:T(128)} %convert_element_type.236, (f32[256,1000]{0,1:T(8,128)}, f32[256,1000]{0,1:T(8,128)}, ...), branch_computations={%region_18.18_spmd, %region_19.22_spmd} | conditional | flops 51247173632 | bytes 353328512 | solution.py:161
  5825.4 276.7 %conditional.10 = (f32[256,1000]{0,1:T(8,128)}, f32[256,1000]{0,1:T(8,128)}, f32[1000,4000]{1,0:T(8,128)}, f32[1000,4000]{1,0:T(8,128)}, f32[4000]{0:T(1024)}, /*index=5*/bf16[1,8,256,1000]{2,3,1,0:T(8,128)(2,1)}) conditional(s32[]{:T(128)} %convert_element_type.236, (f32[256,1000]{0,1:T(8,128)}, f32[256,1000]{0,1:T(8,128)}, ...), branch_computations={%region_18.18_spmd, %region_19.22_spmd} | conditional | flops 51247173632 | bytes 353328512 | solution.py:161
  6245.4 277.7 %conditional.11 = (f32[256,1000]{0,1:T(8,128)}, f32[256,1000]{0,1:T(8,128)}, f32[1000,4000]{1,0:T(8,128)}, f32[1000,4000]{1,0:T(8,128)}, f32[4000]{0:T(1024)}, /*index=5*/bf16[1,8,256,1000]{2,3,1,0:T(8,128)(2,1)}) conditional(s32[]{:T(128)} %convert_element_type.237, (f32[256,1000]{0,1:T(8,128)}, f32[256,1000]{0,1:T(8,128)}, ...), branch_computations={%region_13.13_spmd, %region_14.17_spmd} | conditional | flops 51247173632 | bytes 386096640 | solution.py:161
  6651.5 277.4 %conditional.11 = (f32[256,1000]{0,1:T(8,128)}, f32[256,1000]{0,1:T(8,128)}, f32[1000,4000]{1,0:T(8,128)}, f32[1000,4000]{1,0:T(8,128)}, f32[4000]{0:T(1024)}, /*index=5*/bf16[1,8,256,1000]{2,3,1,0:T(8,128)(2,1)}) conditional(s32[]{:T(128)} %convert_element_type.237, (f32[256,1000]{0,1:T(8,128)}, f32[256,1000]{0,1:T(8,128)}, ...), branch_computations={%region_13.13_spmd, %region_14.17_spmd} | conditional | flops 51247173632 | bytes 386096640 | solution.py:161
  7055.3 277.5 %conditional.11 = (f32[256,1000]{0,1:T(8,128)}, f32[256,1000]{0,1:T(8,128)}, f32[1000,4000]{1,0:T(8,128)}, f32[1000,4000]{1,0:T(8,128)}, f32[4000]{0:T(1024)}, /*index=5*/bf16[1,8,256,1000]{2,3,1,0:T(8,128)(2,1)}) conditional(s32[]{:T(128)} %convert_element_type.237, (f32[256,1000]{0,1:T(8,128)}, f32[256,1000]{0,1:T(8,128)}, ...), branch_computations={%region_13.13_spmd, %region_14.17_spmd} | conditional | flops 51247173632 | bytes 386096640 | solution.py:161
  7459.3 277.7 %conditional.11 = (f32[256,1000]{0,1:T(8,128)}, f32[256,1000]{0,1:T(8,128)}, f32[1000,4000]{1,0:T(8,128)}, f32[1000,4000]{1,0:T(8,128)}, f32[4000]{0:T(1024)}, /*index=5*/bf16[1,8,256,1000]{2,3,1,0:T(8,128)(2,1)}) conditional(s32[]{:T(128)} %convert_element_type.237, (f32[256,1000]{0,1:T(8,128)}, f32[256,1000]{0,1:T(8,128)}, ...), branch_computations={%region_13.13_spmd, %region_14.17_spmd} | conditional | flops 51247173632 | bytes 386096640 | solution.py:161
  (1350 shorter events, 8410.4 us)
Async XLA Ops:
  375.5 90.8 %collective-permute-start.1 = (bf16[2,8,256,1000]{2,3,1,0:T(8,128)(2,1)}, bf16[2,8,256,1000]{2,3,1,0:T(8,128)(2,1)}, u32[]{:S(2)}, u32[]{:S(2)}) collective-permute-start(bf16[2,8,256,1000]{2,3,1,0:T(8,128)(2,1)} %pad_maximum_fusion.9), channel_id=1, source_target_pairs={{0,1},{1,2},{2,3},{3,0},{4,5},{5,6},{6,7},{7,4}} | collective-permute-start | bytes 24576008 | tf_op jit(solution)/shard_map/while/body/eval_jaxpr/ppermute | solution.py:125
  660.7 90.8 %collective-permute-start.1 = (bf16[2,8,256,1000]{2,3,1,0:T(8,128)(2,1)}, bf16[2,8,256,1000]{2,3,1,0:T(8,128)(2,1)}, u32[]{:S(2)}, u32[]{:S(2)}) collective-permute-start(bf16[2,8,256,1000]{2,3,1,0:T(8,128)(2,1)} %pad_maximum_fusion.9), channel_id=1, source_target_pairs={{0,1},{1,2},{2,3},{3,0},{4,5},{5,6},{6,7},{7,4}} | collective-permute-start | bytes 24576008 | tf_op jit(solution)/shard_map/while/body/eval_jaxpr/ppermute | solution.py:125
  946.0 90.8 %collective-permute-start.1 = (bf16[2,8,256,1000]{2,3,1,0:T(8,128)(2,1)}, bf16[2,8,256,1000]{2,3,1,0:T(8,128)(2,1)}, u32[]{:S(2)}, u32[]{:S(2)}) collective-permute-start(bf16[2,8,256,1000]{2,3,1,0:T(8,128)(2,1)} %pad_maximum_fusion.9), channel_id=1, source_target_pairs={{0,1},{1,2},{2,3},{3,0},{4,5},{5,6},{6,7},{7,4}} | collective-permute-start | bytes 24576008 | tf_op jit(solution)/shard_map/while/body/eval_jaxpr/ppermute | solution.py:125
  1231.5 90.8 %collective-permute-start.1 = (bf16[2,8,256,1000]{2,3,1,0:T(8,128)(2,1)}, bf16[2,8,256,1000]{2,3,1,0:T(8,128)(2,1)}, u32[]{:S(2)}, u32[]{:S(2)}) collective-permute-start(bf16[2,8,256,1000]{2,3,1,0:T(8,128)(2,1)} %pad_maximum_fusion.9), channel_id=1, source_target_pairs={{0,1},{1,2},{2,3},{3,0},{4,5},{5,6},{6,7},{7,4}} | collective-permute-start | bytes 24576008 | tf_op jit(solution)/shard_map/while/body/eval_jaxpr/ppermute | solution.py:125
  1520.3 90.8 %collective-permute-start.1 = (bf16[2,8,256,1000]{2,3,1,0:T(8,128)(2,1)}, bf16[2,8,256,1000]{2,3,1,0:T(8,128)(2,1)}, u32[]{:S(2)}, u32[]{:S(2)}) collective-permute-start(bf16[2,8,256,1000]{2,3,1,0:T(8,128)(2,1)} %pad_maximum_fusion.9), channel_id=1, source_target_pairs={{0,1},{1,2},{2,3},{3,0},{4,5},{5,6},{6,7},{7,4}} | collective-permute-start | bytes 24576008 | tf_op jit(solution)/shard_map/while/body/eval_jaxpr/ppermute | solution.py:125
  1808.9 90.8 %collective-permute-start.1 = (bf16[2,8,256,1000]{2,3,1,0:T(8,128)(2,1)}, bf16[2,8,256,1000]{2,3,1,0:T(8,128)(2,1)}, u32[]{:S(2)}, u32[]{:S(2)}) collective-permute-start(bf16[2,8,256,1000]{2,3,1,0:T(8,128)(2,1)} %pad_maximum_fusion.9), channel_id=1, source_target_pairs={{0,1},{1,2},{2,3},{3,0},{4,5},{5,6},{6,7},{7,4}} | collective-permute-start | bytes 24576008 | tf_op jit(solution)/shard_map/while/body/eval_jaxpr/ppermute | solution.py:125
  2097.4 90.8 %collective-permute-start.1 = (bf16[2,8,256,1000]{2,3,1,0:T(8,128)(2,1)}, bf16[2,8,256,1000]{2,3,1,0:T(8,128)(2,1)}, u32[]{:S(2)}, u32[]{:S(2)}) collective-permute-start(bf16[2,8,256,1000]{2,3,1,0:T(8,128)(2,1)} %pad_maximum_fusion.9), channel_id=1, source_target_pairs={{0,1},{1,2},{2,3},{3,0},{4,5},{5,6},{6,7},{7,4}} | collective-permute-start | bytes 24576008 | tf_op jit(solution)/shard_map/while/body/eval_jaxpr/ppermute | solution.py:125
  2386.1 90.8 %collective-permute-start.1 = (bf16[2,8,256,1000]{2,3,1,0:T(8,128)(2,1)}, bf16[2,8,256,1000]{2,3,1,0:T(8,128)(2,1)}, u32[]{:S(2)}, u32[]{:S(2)}) collective-permute-start(bf16[2,8,256,1000]{2,3,1,0:T(8,128)(2,1)} %pad_maximum_fusion.9), channel_id=1, source_target_pairs={{0,1},{1,2},{2,3},{3,0},{4,5},{5,6},{6,7},{7,4}} | collective-permute-start | bytes 24576008 | tf_op jit(solution)/shard_map/while/body/eval_jaxpr/ppermute | solution.py:125
  2494.0 269.0 %collective-permute-start.1 = (bf16[2,8,256,1000]{2,3,1,0:T(8,128)(2,1)}, bf16[2,8,256,1000]{2,3,1,0:T(8,128)(2,1)}, u32[]{:S(2)}, u32[]{:S(2)}) collective-permute-start(bf16[2,8,256,1000]{2,3,1,0:T(8,128)(2,1)} %pad_maximum_fusion.9), channel_id=1, source_target_pairs={{0,1},{1,2},{2,3},{3,0},{4,5},{5,6},{6,7},{7,4}} | collective-permute-start | bytes 24576008 | tf_op jit(solution)/shard_map/while/body/eval_jaxpr/ppermute | solution.py:125
  2780.1 268.9 %collective-permute-start.1 = (bf16[2,8,256,1000]{2,3,1,0:T(8,128)(2,1)}, bf16[2,8,256,1000]{2,3,1,0:T(8,128)(2,1)}, u32[]{:S(2)}, u32[]{:S(2)}) collective-permute-start(bf16[2,8,256,1000]{2,3,1,0:T(8,128)(2,1)} %pad_maximum_fusion.9), channel_id=1, source_target_pairs={{0,1},{1,2},{2,3},{3,0},{4,5},{5,6},{6,7},{7,4}} | collective-permute-start | bytes 24576008 | tf_op jit(solution)/shard_map/while/body/eval_jaxpr/ppermute | solution.py:125
  3066.1 269.1 %collective-permute-start.1 = (bf16[2,8,256,1000]{2,3,1,0:T(8,128)(2,1)}, bf16[2,8,256,1000]{2,3,1,0:T(8,128)(2,1)}, u32[]{:S(2)}, u32[]{:S(2)}) collective-permute-start(bf16[2,8,256,1000]{2,3,1,0:T(8,128)(2,1)} %pad_maximum_fusion.9), channel_id=1, source_target_pairs={{0,1},{1,2},{2,3},{3,0},{4,5},{5,6},{6,7},{7,4}} | collective-permute-start | bytes 24576008 | tf_op jit(solution)/shard_map/while/body/eval_jaxpr/ppermute | solution.py:125
  3452.2 350.5 %collective-permute-start = (bf16[2,8,256,1000]{2,3,1,0:T(8,128)(2,1)}, bf16[2,8,256,1000]{2,3,1,0:T(8,128)(2,1)}, u32[]{:S(2)}, u32[]{:S(2)}) collective-permute-start(bf16[2,8,256,1000]{2,3,1,0:T(8,128)(2,1)} %pad_maximum_fusion.10), channel_id=1, source_target_pairs={{0,3},{1,0},{2,1},{3,2},{4,7},{5,4},{6,5},{7,6}} | collective-permute-start | bytes 24576008 | tf_op jit(solution)/shard_map/while/body/eval_jaxpr/ppermute | solution.py:164
  3848.0 353.1 %collective-permute-start = (bf16[2,8,256,1000]{2,3,1,0:T(8,128)(2,1)}, bf16[2,8,256,1000]{2,3,1,0:T(8,128)(2,1)}, u32[]{:S(2)}, u32[]{:S(2)}) collective-permute-start(bf16[2,8,256,1000]{2,3,1,0:T(8,128)(2,1)} %pad_maximum_fusion.10), channel_id=1, source_target_pairs={{0,3},{1,0},{2,1},{3,2},{4,7},{5,4},{6,5},{7,6}} | collective-permute-start | bytes 24576008 | tf_op jit(solution)/shard_map/while/body/eval_jaxpr/ppermute | solution.py:164
  4246.0 353.2 %collective-permute-start = (bf16[2,8,256,1000]{2,3,1,0:T(8,128)(2,1)}, bf16[2,8,256,1000]{2,3,1,0:T(8,128)(2,1)}, u32[]{:S(2)}, u32[]{:S(2)}) collective-permute-start(bf16[2,8,256,1000]{2,3,1,0:T(8,128)(2,1)} %pad_maximum_fusion.10), channel_id=1, source_target_pairs={{0,3},{1,0},{2,1},{3,2},{4,7},{5,4},{6,5},{7,6}} | collective-permute-start | bytes 24576008 | tf_op jit(solution)/shard_map/while/body/eval_jaxpr/ppermute | solution.py:164
  4906.7 90.7 %collective-permute-start = (bf16[2,8,256,1000]{2,3,1,0:T(8,128)(2,1)}, bf16[2,8,256,1000]{2,3,1,0:T(8,128)(2,1)}, u32[]{:S(2)}, u32[]{:S(2)}) collective-permute-start(bf16[2,8,256,1000]{2,3,1,0:T(8,128)(2,1)} %pad_maximum_fusion.10), channel_id=1, source_target_pairs={{0,3},{1,0},{2,1},{3,2},{4,7},{5,4},{6,5},{7,6}} | collective-permute-start | bytes 24576008 | tf_op jit(solution)/shard_map/while/body/eval_jaxpr/ppermute | solution.py:164
  5305.0 98.6 %collective-permute-start = (bf16[2,8,256,1000]{2,3,1,0:T(8,128)(2,1)}, bf16[2,8,256,1000]{2,3,1,0:T(8,128)(2,1)}, u32[]{:S(2)}, u32[]{:S(2)}) collective-permute-start(bf16[2,8,256,1000]{2,3,1,0:T(8,128)(2,1)} %pad_maximum_fusion.10), channel_id=1, source_target_pairs={{0,3},{1,0},{2,1},{3,2},{4,7},{5,4},{6,5},{7,6}} | collective-permute-start | bytes 24576008 | tf_op jit(solution)/shard_map/while/body/eval_jaxpr/ppermute | solution.py:164
  5710.9 98.4 %collective-permute-start = (bf16[2,8,256,1000]{2,3,1,0:T(8,128)(2,1)}, bf16[2,8,256,1000]{2,3,1,0:T(8,128)(2,1)}, u32[]{:S(2)}, u32[]{:S(2)}) collective-permute-start(bf16[2,8,256,1000]{2,3,1,0:T(8,128)(2,1)} %pad_maximum_fusion.10), channel_id=1, source_target_pairs={{0,3},{1,0},{2,1},{3,2},{4,7},{5,4},{6,5},{7,6}} | collective-permute-start | bytes 24576008 | tf_op jit(solution)/shard_map/while/body/eval_jaxpr/ppermute | solution.py:164
  6116.7 98.4 %collective-permute-start = (bf16[2,8,256,1000]{2,3,1,0:T(8,128)(2,1)}, bf16[2,8,256,1000]{2,3,1,0:T(8,128)(2,1)}, u32[]{:S(2)}, u32[]{:S(2)}) collective-permute-start(bf16[2,8,256,1000]{2,3,1,0:T(8,128)(2,1)} %pad_maximum_fusion.10), channel_id=1, source_target_pairs={{0,3},{1,0},{2,1},{3,2},{4,7},{5,4},{6,5},{7,6}} | collective-permute-start | bytes 24576008 | tf_op jit(solution)/shard_map/while/body/eval_jaxpr/ppermute | solution.py:164
  6449.6 49.2 slice-start
  6530.5 90.8 %collective-permute-start = (bf16[2,8,256,1000]{2,3,1,0:T(8,128)(2,1)}, bf16[2,8,256,1000]{2,3,1,0:T(8,128)(2,1)}, u32[]{:S(2)}, u32[]{:S(2)}) collective-permute-start(bf16[2,8,256,1000]{2,3,1,0:T(8,128)(2,1)} %pad_maximum_fusion.10), channel_id=1, source_target_pairs={{0,3},{1,0},{2,1},{3,2},{4,7},{5,4},{6,5},{7,6}} | collective-permute-start | bytes 24576008 | tf_op jit(solution)/shard_map/while/body/eval_jaxpr/ppermute | solution.py:164
  6936.3 88.8 %collective-permute-start = (bf16[2,8,256,1000]{2,3,1,0:T(8,128)(2,1)}, bf16[2,8,256,1000]{2,3,1,0:T(8,128)(2,1)}, u32[]{:S(2)}, u32[]{:S(2)}) collective-permute-start(bf16[2,8,256,1000]{2,3,1,0:T(8,128)(2,1)} %pad_maximum_fusion.10), channel_id=1, source_target_pairs={{0,3},{1,0},{2,1},{3,2},{4,7},{5,4},{6,5},{7,6}} | collective-permute-start | bytes 24576008 | tf_op jit(solution)/shard_map/while/body/eval_jaxpr/ppermute | solution.py:164
  7340.2 88.8 %collective-permute-start = (bf16[2,8,256,1000]{2,3,1,0:T(8,128)(2,1)}, bf16[2,8,256,1000]{2,3,1,0:T(8,128)(2,1)}, u32[]{:S(2)}, u32[]{:S(2)}) collective-permute-start(bf16[2,8,256,1000]{2,3,1,0:T(8,128)(2,1)} %pad_maximum_fusion.10), channel_id=1, source_target_pairs={{0,3},{1,0},{2,1},{3,2},{4,7},{5,4},{6,5},{7,6}} | collective-permute-start | bytes 24576008 | tf_op jit(solution)/shard_map/while/body/eval_jaxpr/ppermute | solution.py:164
  7663.5 49.2 slice-start
  7744.4 88.8 %collective-permute-start = (bf16[2,8,256,1000]{2,3,1,0:T(8,128)(2,1)}, bf16[2,8,256,1000]{2,3,1,0:T(8,128)(2,1)}, u32[]{:S(2)}, u32[]{:S(2)}) collective-permute-start(bf16[2,8,256,1000]{2,3,1,0:T(8,128)(2,1)} %pad_maximum_fusion.10), channel_id=1, source_target_pairs={{0,3},{1,0},{2,1},{3,2},{4,7},{5,4},{6,5},{7,6}} | collective-permute-start | bytes 24576008 | tf_op jit(solution)/shard_map/while/body/eval_jaxpr/ppermute | solution.py:164
  (163 other events, 922.8 us)
where the time goes:
time: 7910 us; the launch traced here: 7890 us
  waiting for transfers between devices  2410 us (30%)
  matrix products  1870 us (24%)
  other arithmetic  1370 us (17%)
  local copies, waits for them, and re-layouts  1200 us (15%)
  starting transfers between devices  926 us (12%)
  loops' own time  107 us (1%)
    ppermute x11, waiting for transfers between devices, fwd_tick(): inbox = lax.ppermute(jnp.stack(outbox), 'pp', fwd_perm)  1430 us
    ppermute x11, waiting for transfers between devices, bwd_tick(): inbox = lax.ppermute(jnp.stack(outbox), 'pp', bwd_perm)  977 us
    ppermute x11, starting transfers between devices, bwd_tick(): inbox = lax.ppermute(jnp.stack(outbox), 'pp', bwd_perm)  823 us
    dot_general x64, matrix products, cell_step(): jnp.dot(h_prev, w_hid, preferred_element_type=jnp.float32)  645 us
    dot_general x64, matrix products, step_fn(): jnp.einsum('bg,hg->bh', grad_low, w_hid, preferred_element_type=jnp.float32)  445 us
    concatenate x128, other arithmetic, cell_grad(): jnp.concatenate([dc_total * gate_g * gate_i * (1.0 - gate_i), dc_total *...  393 us
    dynamic_update_slice x20, local copies, waits for them, and re-layouts, place(): return lax.dynamic_update_slice_in_dim(buf, piece, start, 0)  267 us
    dynamic_slice x16, local copies, waits for them, and re-layouts, window_of(): return lax.dynamic_slice_in_dim(buf, start, SPAN_STEPS, 0)  235 us
  transfers between devices with their start and end apart: 22, of which 22 were waited for; matrix products, arithmetic and copies ran while one was open for 0% of the time, Pallas kernels for 0%

commit v1 on v0

v1 whole, which is shorter than its diff:
```python
import functools

import jax
import jax.numpy as jnp
from jax import lax
from jax.experimental import pallas as pl
from jax.experimental.pallas import tpu as pltpu
from jax.sharding import PartitionSpec as P

F32 = jnp.float32
BF16 = jnp.bfloat16
MESH = pl.DeviceIdType.MESH
BLK = 256
ROWS = 16
VMEM_LIMIT = 67043328


def _sigmoid(v):
    return 0.5 * jnp.tanh(0.5 * v) + 0.5


def _enter(n_stages):
    stage = lax.axis_index('pp')
    nxt = lax.rem(stage + 1, n_stages)
    prv = lax.rem(stage + n_stages - 1, n_stages)
    barrier = pltpu.get_barrier_semaphore()
    for peer in (nxt, prv):
        pl.semaphore_signal(barrier, inc=1, device_id={'pp': peer}, device_id_type=MESH)
    pl.semaphore_wait(barrier, 2)
    return stage, nxt, prv


def _fwd_kernel(n_stages, n_steps, n_blk, seq0, wx_hbm, wh_hbm, bias, h0, c0, landing, r_t, h_t, gates, cells, top, wx, wh, xb0, xb1, hb0, hb1, cb0, cb1, gb0, gb1, ob0, ob1, xt0, xt1, ht0, ht1, w_sem, x_sem, g_sem, c_sem, o_sem, xt_sem, ht_sem, i_sem, recv_sem):
    stage, nxt, _ = _enter(n_stages)
    n_total = 2 * n_steps
    xb, hb, cb, gb, ob = (xb0, xb1), (hb0, hb1), (cb0, cb1), (gb0, gb1), (ob0, ob1)
    xt, ht = (xt0, xt1), (ht0, ht1)
    is_first = stage == 0
    is_last = stage == n_stages - 1

    def weight_copies(k):
        return [pltpu.make_async_copy(wx_hbm.at[k], wx.at[k], w_sem.at[2 * k]), pltpu.make_async_copy(wh_hbm.at[k], wh.at[k], w_sem.at[2 * k + 1])]

    for k in range(2):
        for copy in weight_copies(k):
            copy.start()

    def landed(n):
        k, t = n // n_steps, lax.rem(n, n_steps)
        return pltpu.make_async_remote_copy(src_ref=ob0, dst_ref=landing.at[k, t], send_sem=o_sem.at[0, 0], recv_sem=recv_sem.at[n], device_id={'pp': nxt}, device_id_type=MESH)

    def fetch(n, u):
        k, t = n // n_steps, lax.rem(n, n_steps)
        from_args = is_first & (k == 0)

        @pl.when(from_args)
        def _():
            pltpu.make_async_copy(seq0.at[t], xb[u], x_sem.at[u]).start()

        @pl.when(jnp.logical_not(from_args))
        def _():
            landed(n).wait_recv()
            pltpu.make_async_copy(landing.at[k, t], xb[u], x_sem.at[u]).start()

    def cols(j):
        return pl.ds(j * BLK, BLK)

    def send(n, u, j):
        k, t = n // n_steps, lax.rem(n, n_steps)
        k_next = jnp.minimum(k + stage // (n_stages - 1), 1)
        return pltpu.make_async_remote_copy(src_ref=ob[u].at[:, cols(j)], dst_ref=landing.at[k_next, t, :, cols(j)], send_sem=o_sem.at[u, j], recv_sem=recv_sem.at[k_next * n_steps + t], device_id={'pp': nxt}, device_id_type=MESH)

    def keep(n, u, j):
        return pltpu.make_async_copy(ob[u].at[:, cols(j)], top.at[lax.rem(n, n_steps), :, cols(j)], o_sem.at[u, j])

    def cell_copy(n, u):
        return pltpu.make_async_copy(cb[u], cells.at[n // n_steps, lax.rem(n, n_steps) + 1], c_sem.at[u])

    def out_copies(n, u):
        k, t = n // n_steps, lax.rem(n, n_steps)
        return [pltpu.make_async_copy(gb[u].at[j], gates.at[k, t, j], g_sem.at[u, j]) for j in range(n_blk)] + [cell_copy(n, u), pltpu.make_async_copy(xt[u], r_t.at[k, t], xt_sem.at[u]), pltpu.make_async_copy(ht[u], h_t.at[k, t], ht_sem.at[u])]

    def wait_outs(n, u):
        for copy in out_copies(n, u):
            copy.wait()
        at_top = is_last & (n // n_steps == 1)

        @pl.when(at_top)
        def _():
            for j in range(n_blk):
                keep(n, u, j).wait()

        @pl.when(jnp.logical_not(at_top))
        def _():
            for j in range(n_blk):
                send(n, u, j).wait_send()

    fetch(0, 0)

    def step(n, u):
        k, t = n // n_steps, lax.rem(n, n_steps)
        v = 1 - u
        if u == 0:

            @pl.when(t == 0)
            def _():
                for copy in weight_copies(k):
                    copy.wait()

                @pl.when(n > 0)
                def _():
                    cell_copy(n - 1, v).wait()

                h_in = pltpu.make_async_copy(h0.at[k], hb[v], i_sem.at[0])
                c_in = pltpu.make_async_copy(c0.at[k], cb[v], i_sem.at[1])
                h_in.start()
                c_in.start()
                h_in.wait()
                c_in.wait()
                pltpu.make_async_copy(cb[v], cells.at[k, 0], c_sem.at[v]).start()

        else:

            @pl.when(n == 1)
            def _():
                cell_copy(n, u).wait()

        @pl.when(n >= 2)
        def _():
            wait_outs(n - 2, u)

        pltpu.make_async_copy(seq0.at[0], xb[u], x_sem.at[u]).wait()
        for j in range(n_blk):
            z = jnp.dot(xb[u][...], wx[k, j], preferred_element_type=F32) + jnp.dot(hb[v][...], wh[k, j], preferred_element_type=F32)
            gb[u][j] = z + bias[k, j]
            for r in range(0, BLK, ROWS):
                rows = pl.ds(r, ROWS)
                gate_i = _sigmoid(gb[u][j, rows, 0:BLK])
                gate_f = _sigmoid(gb[u][j, rows, BLK:2 * BLK])
                gate_g = jnp.tanh(gb[u][j, rows, 2 * BLK:3 * BLK])
                gate_o = _sigmoid(gb[u][j, rows, 3 * BLK:4 * BLK])
                c_new = gate_f * cb[v][rows, cols(j)] + gate_i * gate_g
                h_new = (gate_o * jnp.tanh(c_new)).astype(BF16)
                gb[u][j, rows, 0:BLK] = gate_i
                gb[u][j, rows, BLK:2 * BLK] = gate_f
                gb[u][j, rows, 2 * BLK:3 * BLK] = gate_g
                gb[u][j, rows, 3 * BLK:4 * BLK] = gate_o
                cb[u][rows, cols(j)] = c_new
                hb[u][rows, cols(j)] = h_new
                ob[u][rows, cols(j)] = (xb[u][rows, cols(j)].astype(F32) + h_new.astype(F32)).astype(BF16)
            xt[u][cols(j), :] = xb[u][:, cols(j)].T
            ht[u][cols(j), :] = hb[v][:, cols(j)].T
            if j == n_blk - 2:

                @pl.when(n + 1 < n_total)
                def _():
                    fetch(n + 1, v)

        at_top = is_last & (k == 1)

        @pl.when(at_top)
        def _():
            for j in range(n_blk):
                keep(n, u, j).start()

        @pl.when(jnp.logical_not(at_top))
        def _():
            for j in range(n_blk):
                send(n, u, j).start()

        for copy in out_copies(n, u):
            copy.start()

    def pair(i, carry):
        step(2 * i, 0)
        step(2 * i + 1, 1)
        return carry

    lax.fori_loop(0, n_steps, pair, 0)
    wait_outs(n_total - 2, 0)
    wait_outs(n_total - 1, 1)


def _bwd_kernel(n_stages, n_steps, n_blk, scale, gates, cells, h_t, top, target, wx_hbm, wh_hbm, landing, dz_seq, dwh, db, dh_out, dc_out, loss, wx, wh, acc, zb0, zb1, gb0, gb1, cb0, cb1, ab0, ab1, tb0, tb1, ob0, ob1, hb0, hb1, dh, dc, bacc, lacc, w_sem, g_sem, c_sem, a_sem, t_sem, h_sem, z_sem, o_sem, f_sem, recv_sem):
    stage, nxt, prv = _enter(n_stages)
    n_total = 2 * n_steps
    zb, gb, cb, ab, tb, ob, hb = (zb0, zb1), (gb0, gb1), (cb0, cb1), (ab0, ab1), (tb0, tb1), (ob0, ob1), (hb0, hb1)
    is_first = stage == 0
    is_last = stage == n_stages - 1

    def weight_copies(k):
        return [pltpu.make_async_copy(wx_hbm.at[k], wx, w_sem.at[0]), pltpu.make_async_copy(wh_hbm.at[k], wh, w_sem.at[1])]

    for copy in weight_copies(1):
        copy.start()

    def place(n):
        return 1 - n // n_steps, n_steps - 1 - lax.rem(n, n_steps)

    def cols(j):
        return pl.ds(j * BLK, BLK)

    def landed(n):
        k, t = place(n)
        return pltpu.make_async_remote_copy(src_ref=ob0, dst_ref=landing.at[k, t], send_sem=o_sem.at[0, 0], recv_sem=recv_sem.at[n], device_id={'pp': prv}, device_id_type=MESH)

    def fetch_saved(n, u):
        k, t = place(n)
        for j in range(n_blk):
            pltpu.make_async_copy(gates.at[k, t, j], gb[u].at[j], g_sem.at[u, j]).start()
        pltpu.make_async_copy(cells.at[k, pl.ds(t, 2)], cb[u], c_sem.at[u]).start()
        pltpu.make_async_copy(h_t.at[k, t], hb[u], h_sem.at[u]).start()

    def wait_saved(u):
        for j in range(n_blk):
            pltpu.make_async_copy(gates.at[0, 0, j], gb[u].at[j], g_sem.at[u, j]).wait()
        pltpu.make_async_copy(cells.at[0, pl.ds(0, 2)], cb[u], c_sem.at[u]).wait()

    def wait_h(u):
        pltpu.make_async_copy(h_t.at[0, 0], hb[u], h_sem.at[u]).wait()

    def fetch_grad(n, u):
        k, t = place(n)
        at_top = is_last & (k == 1)

        @pl.when(at_top)
        def _():
            pltpu.make_async_copy(top.at[t], ab[u], a_sem.at[u]).start()
            pltpu.make_async_copy(target.at[t], tb[u], t_sem.at[u]).start()

        @pl.when(jnp.logical_not(at_top))
        def _():
            landed(n).wait_recv()
            pltpu.make_async_copy(landing.at[k, t], ab[u], a_sem.at[u]).start()

    def wait_grad(n, u):
        pltpu.make_async_copy(top.at[0], ab[u], a_sem.at[u]).wait()

        @pl.when(is_last & (n // n_steps == 0))
        def _():
            pltpu.make_async_copy(target.at[0], tb[u], t_sem.at[u]).wait()

    def send(n, u, j):
        k, t = place(n)
        k_next = jnp.maximum(k - (n_stages - 1 - stage) // (n_stages - 1), 0)
        n_next = (1 - k_next) * n_steps + lax.rem(n, n_steps)
        return pltpu.make_async_remote_copy(src_ref=ob[u].at[:, cols(j)], dst_ref=landing.at[k_next, t, :, cols(j)], send_sem=o_sem.at[u, j], recv_sem=recv_sem.at[n_next], device_id={'pp': prv}, device_id_type=MESH)

    def sends(n):
        return jnp.logical_not(is_first & (n // n_steps == 1))

    def dz_copies(n, u):
        k, t = place(n)
        return [pltpu.make_async_copy(zb[u].at[j], dz_seq.at[k, t, j], z_sem.at[u, j]) for j in range(n_blk)]

    def wait_outs(n, u):
        for copy in dz_copies(n, u):
            copy.wait()

        @pl.when(sends(n))
        def _():
            for j in range(n_blk):
                send(n, u, j).wait_send()

    def weight_grad(v, j):
        acc[j] += jnp.dot(hb[v][...], zb[v][j], preferred_element_type=F32)

    acc_copies = lambda k: [pltpu.make_async_copy(acc, dwh.at[k], f_sem.at[0]), pltpu.make_async_copy(dh, dh_out.at[k], f_sem.at[1]), pltpu.make_async_copy(dc, dc_out.at[k], f_sem.at[2]), pltpu.make_async_copy(bacc, db.at[k], f_sem.at[3])]

    def begin_round():
        acc[...] = jnp.zeros_like(acc)
        dh[...] = jnp.zeros_like(dh)
        dc[...] = jnp.zeros_like(dc)
        bacc[...] = jnp.zeros_like(bacc)
        tb0[...] = jnp.zeros_like(tb0)
        tb1[...] = jnp.zeros_like(tb1)
        zb1[...] = jnp.zeros_like(zb1)

    def end_round(k, n_last):
        wait_h(1)
        for j in range(n_blk):
            weight_grad(1, j)
        for copy in acc_copies(k):
            copy.start()
        for copy in acc_copies(k):
            copy.wait()

    begin_round()
    lacc[...] = jnp.zeros_like(lacc)
    fetch_saved(0, 0)
    fetch_grad(0, 0)
    hb1[...] = jnp.zeros_like(hb1)
    for copy in weight_copies(1):
        copy.wait()

    def step(n, u):
        k, t = place(n)
        v = 1 - u
        if u == 0:

            @pl.when(n == n_steps)
            def _():
                wait_h(1)
                for j in range(n_blk):
                    weight_grad(1, j)
                for copy in weight_copies(0):
                    copy.start()
                wait_outs(n - 1, 1)
                for copy in acc_copies(1):
                    copy.start()
                for copy in acc_copies(1):
                    copy.wait()
                begin_round()
                hb1[...] = jnp.zeros_like(hb1)
                for copy in weight_copies(0):
                    copy.wait()

        if u == 0:

            @pl.when((n >= 2) & (n != n_steps))
            def _():
                wait_h(v)
                wait_outs(n - 2, u)

            @pl.when(n == n_steps)
            def _():
                wait_outs(n - 2, u)
        else:
            wait_h(v)

            @pl.when((n >= 2) & (n != n_steps + 1))
            def _():
                wait_outs(n - 2, u)

            @pl.when(n == n_steps + 1)
            def _():
                pass

        wait_saved(u)
        wait_grad(n, u)
        mult = jnp.where(is_last & (k == 1), scale, 1.0).astype(F32)
        for j in range(n_blk):
            weight_grad(v, j)
            for r in range(0, BLK, ROWS):
                rows = pl.ds(r, ROWS)
                gate_i = gb[u][j, rows, 0:BLK]
                gate_f = gb[u][j, rows, BLK:2 * BLK]
                gate_g = gb[u][j, rows, 2 * BLK:3 * BLK]
                gate_o = gb[u][j, rows, 3 * BLK:4 * BLK]
                c_prev = cb[u][0, rows, cols(j)]
                tanh_c = jnp.tanh(cb[u][1, rows, cols(j)])
                diff = ab[u][rows, cols(j)].astype(F32) - tb[u][rows, cols(j)].astype(F32)
                lacc[:, cols(j)] += diff[0:8] * diff[0:8] + diff[8:16] * diff[8:16]
                dh_all = diff * mult + dh[rows, cols(j)]
                dho = dh_all * gate_o
                dc_all = dc[rows, cols(j)] + dho * (1.0 - tanh_c * tanh_c)
                dz_i = dc_all * gate_g * gate_i * (1.0 - gate_i)
                dz_f = dc_all * c_prev * gate_f * (1.0 - gate_f)
                dz_g = dc_all * gate_i * (1.0 - gate_g * gate_g)
                dz_o = dho * tanh_c * (1.0 - gate_o)
                dc[rows, cols(j)] = dc_all * gate_f
                for g, dz in enumerate((dz_i, dz_f, dz_g, dz_o)):
                    bacc[j, :, g * BLK:(g + 1) * BLK] += dz[0:8] + dz[8:16]
                    zb[u][j, rows, g * BLK:(g + 1) * BLK] = dz.astype(BF16)
        for copy in dz_copies(n, u):
            copy.start()
        contract = (((1,), (1,)), ((), ()))
        for i in range(n_blk):
            dh[:, cols(i)] = sum(lax.dot_general(zb[u][j], wh[j, cols(i), :], contract, preferred_element_type=F32) for j in range(n_blk))

        @pl.when(n + 1 < n_total)
        def _():
            fetch_saved(n + 1, v)
            fetch_grad(n + 1, v)

        for i in range(n_blk):
            part = sum(lax.dot_general(zb[u][j], wx[j, cols(i), :], contract, preferred_element_type=F32) for j in range(n_blk))
            into = (ab[u][:, cols(i)].astype(F32) - tb[u][:, cols(i)].astype(F32)) * mult
            ob[u][:, cols(i)] = (into + part).astype(BF16)

        @pl.when(sends(n))
        def _():
            for i in range(n_blk):
                send(n, u, i).start()

        @pl.when(n == n_steps - 1)
        def _():
            out = pltpu.make_async_copy(lacc, loss, f_sem.at[0])
            out.start()
            out.wait()

    def pair(i, carry):
        step(2 * i, 0)
        step(2 * i + 1, 1)
        return carry

    lax.fori_loop(0, n_steps, pair, 0)
    wait_outs(n_total - 2, 0)
    wait_outs(n_total - 1, 1)
    end_round(0, n_total - 1)


def _natural(n_hid, n_blk, src, dst):
    for g in range(4):
        for j in range(n_blk):
            width = min(BLK, n_hid - j * BLK)
            dst[:, g * n_hid + j * BLK:g * n_hid + j * BLK + width] = src(j, g)[:, :width]


def _dense_kernel(n_hid, n_blk, n_chunk, r_ref, z_ref, packed_ref, dwx_ref, dwh_ref, acc):
    chunk = pl.program_id(2)

    @pl.when(chunk == 0)
    def _():
        acc[...] = jnp.zeros_like(acc)

    for j in range(n_blk):
        acc[j] += sum(jnp.dot(r_ref[0, t], z_ref[0, t, j], preferred_element_type=F32) for t in range(n_chunk))
    _natural(n_hid, n_blk, lambda j, g: packed_ref[0, j, :, g * BLK:(g + 1) * BLK], dwh_ref.at[0])

    @pl.when(chunk == pl.num_programs(2) - 1)
    def _():
        _natural(n_hid, n_blk, lambda j, g: acc[j, :, g * BLK:(g + 1) * BLK], dwx_ref.at[0])


def solution(mesh):
    n_stages = mesh.shape['pp']

    def local_fn(inputs, targets, w_in, w_hid, bias, h_init, c_init):
        n_batch, n_steps, n_hid = inputs.shape
        n_blk = -(-n_hid // BLK)
        n_pad = n_blk * BLK
        extra = n_pad - n_hid
        stage = lax.axis_index('pp')

        def time_major(seq):
            return jnp.pad(jnp.swapaxes(seq, 0, 1), ((0, 0), (0, 0), (0, extra)))

        def pack(w):
            lead, rows = w.shape[0], w.shape[1]
            parts = jnp.pad(w.reshape(lead, rows, 4, n_hid), ((0, 0), (0, (-rows) % BLK if rows > 1 else 0), (0, 0), (0, extra)))
            parts = parts.reshape(lead, parts.shape[1], 4, n_blk, BLK)
            return jnp.transpose(parts, (0, 3, 1, 2, 4)).reshape(lead, n_blk, parts.shape[1], 4 * BLK)

        seq0 = time_major(inputs)
        target = time_major(targets)
        wx_p, wh_p = pack(w_in[:, 0]), pack(w_hid[:, 0])
        bias_p = pack(bias)
        h0 = jnp.pad(h_init[:, 0], ((0, 0), (0, 0), (0, extra))).astype(BF16)
        c0 = jnp.pad(c_init[:, 0], ((0, 0), (0, 0), (0, extra)))

        def shape(*dims, dtype=BF16):
            return jax.ShapeDtypeStruct(dims, dtype)

        any_spec = pl.BlockSpec(memory_space=pl.ANY)
        vmem_spec = pl.BlockSpec(memory_space=pltpu.VMEM)
        row = (n_batch, n_pad)
        dma = pltpu.SemaphoreType.DMA
        step_flops = 2 * n_batch * n_pad * 4 * n_pad
        _, r_t, h_t, gates, cells, top = pl.pallas_call(
            functools.partial(_fwd_kernel, n_stages, n_steps, n_blk),
            out_shape=(shape(2, n_steps, *row), shape(2, n_steps, n_pad, n_batch), shape(2, n_steps, n_pad, n_batch), shape(2, n_steps, n_blk, n_batch, 4 * BLK, dtype=F32), shape(2, n_steps + 1, *row, dtype=F32), shape(n_steps, *row)),
            in_specs=[any_spec, any_spec, any_spec, vmem_spec, any_spec, any_spec],
            out_specs=[any_spec] * 6,
            scratch_shapes=[pltpu.VMEM((2, n_blk, n_pad, 4 * BLK), BF16)] * 2 + [pltpu.VMEM(row, BF16)] * 4 + [pltpu.VMEM(row, F32)] * 2 + [pltpu.VMEM((n_blk, n_batch, 4 * BLK), F32)] * 2 + [pltpu.VMEM(row, BF16)] * 2 + [pltpu.VMEM((n_pad, n_batch), BF16)] * 4 + [dma((4,)), dma((2,)), dma((2, n_blk)), dma((2,)), dma((2, n_blk)), dma((2,)), dma((2,)), dma((2,)), dma((2 * n_steps,))],
            compiler_params=pltpu.CompilerParams(collective_id=0, has_side_effects=True, vmem_limit_bytes=VMEM_LIMIT),
            cost_estimate=pl.CostEstimate(flops=4 * n_steps * step_flops, bytes_accessed=0, transcendentals=0),
            name='lstm_forward',
        )(seq0, wx_p, wh_p, bias_p, h0, c0)

        scale = 1.0 / (n_batch * n_steps)
        _, dz_seq, dwh_p, db_p, dh_p, dc_p, loss_p = pl.pallas_call(
            functools.partial(_bwd_kernel, n_stages, n_steps, n_blk, scale),
            out_shape=(shape(2, n_steps, *row), shape(2, n_steps, n_blk, n_batch, 4 * BLK), shape(2, n_blk, n_pad, 4 * BLK, dtype=F32), shape(2, n_blk, 8, 4 * BLK, dtype=F32), shape(2, *row, dtype=F32), shape(2, *row, dtype=F32), shape(8, n_pad, dtype=F32)),
            in_specs=[any_spec] * 7,
            out_specs=[any_spec] * 7,
            scratch_shapes=[pltpu.VMEM((n_blk, n_pad, 4 * BLK), BF16)] * 2 + [pltpu.VMEM((n_blk, n_pad, 4 * BLK), F32)] + [pltpu.VMEM((n_blk, n_batch, 4 * BLK), BF16)] * 2 + [pltpu.VMEM((n_blk, n_batch, 4 * BLK), F32)] * 2 + [pltpu.VMEM((2, *row), F32)] * 2 + [pltpu.VMEM(row, BF16)] * 6 + [pltpu.VMEM((n_pad, n_batch), BF16)] * 2 + [pltpu.VMEM(row, F32)] * 2 + [pltpu.VMEM((n_blk, 8, 4 * BLK), F32), pltpu.VMEM((8, n_pad), F32)] + [dma((2,)), dma((2, n_blk)), dma((2,)), dma((2,)), dma((2,)), dma((2,)), dma((2, n_blk)), dma((2, n_blk)), dma((4,)), dma((2 * n_steps,))],
            compiler_params=pltpu.CompilerParams(collective_id=1, has_side_effects=True, vmem_limit_bytes=VMEM_LIMIT),
            cost_estimate=pl.CostEstimate(flops=6 * n_steps * step_flops, bytes_accessed=0, transcendentals=0),
            name='lstm_backward',
        )(gates, cells, h_t, top, target, wx_p, wh_p)

        n_chunk = 4
        m_rows = 512
        m_tiles = n_pad // m_rows
        per_round = m_tiles * (n_steps // n_chunk)
        p_rows = n_pad // per_round
        part = lambda k, m, c: m * (n_steps // n_chunk) + c
        dwx, dwh = pl.pallas_call(
            functools.partial(_dense_kernel, n_hid, n_blk, n_chunk),
            grid=(2, m_tiles, n_steps // n_chunk),
            out_shape=(shape(2, n_hid, 4 * n_hid, dtype=F32), shape(2, n_hid, 4 * n_hid, dtype=F32)),
            in_specs=[pl.BlockSpec((1, n_chunk, m_rows, n_batch), lambda k, m, c: (k, c, m, 0)), pl.BlockSpec((1, n_chunk, n_blk, n_batch, 4 * BLK), lambda k, m, c: (k, c, 0, 0, 0)), pl.BlockSpec((1, n_blk, p_rows, 4 * BLK), lambda k, m, c: (k, 0, part(k, m, c), 0))],
            out_specs=[pl.BlockSpec((1, m_rows, 4 * n_hid), lambda k, m, c: (k, m, 0)), pl.BlockSpec((1, p_rows, 4 * n_hid), lambda k, m, c: (k, part(k, m, c), 0))],
            scratch_shapes=[pltpu.VMEM((n_blk, m_rows, 4 * BLK), F32)],
            compiler_params=pltpu.CompilerParams(dimension_semantics=('arbitrary', 'arbitrary', 'arbitrary'), vmem_limit_bytes=VMEM_LIMIT),
            cost_estimate=pl.CostEstimate(flops=2 * n_steps * step_flops, bytes_accessed=0, transcendentals=0),
            name='input_weight_grad',
        )(r_t, dz_seq, dwh_p)

        local_loss = jnp.where(stage == n_stages - 1, 0.5 * scale * jnp.sum(loss_p), 0.0)
        loss = lax.psum(local_loss, 'pp')
        db = jnp.sum(db_p, axis=2).reshape(2, n_blk, 4, BLK)
        db = jnp.transpose(db, (0, 2, 1, 3)).reshape(2, 4, n_pad)[:, :, :n_hid].reshape(2, 4 * n_hid)
        return loss[None], dwx[:, None], dwh[:, None], db[:, None], dh_p[:, None, :, :n_hid], dc_p[:, None, :, :n_hid]

    spec_seq = P('dp', None, None)
    spec_weight = P('dp', 'pp', None, None)
    spec_bias = P('dp', 'pp', None)
    return jax.shard_map(local_fn, mesh=mesh, in_specs=(spec_seq, spec_seq, spec_weight, spec_weight, spec_bias, spec_weight, spec_weight), out_specs=(P('dp'), spec_weight, spec_weight, spec_bias, spec_weight, spec_weight), check_vma=False)
```

time: 7910 us -> 1470 us (0.19)
  waiting for transfers between devices: 2410 us -> 0 us
  matrix products: 1870 us -> 0 us
  other arithmetic: 1370 us -> 0.77 us
  Pallas kernels: 0 us -> 1190 us
  local copies, waits for them, and re-layouts: 1200 us -> 267 us
  starting transfers between devices: 926 us -> 0 us
  loops' own time: 107 us -> 0 us
    ppermute x22 -> x0, waiting for transfers between devices: 2410 us -> none  [the longest x11 1430 us: fwd_tick(): inbox = lax.ppermute(jnp.stack(outbox), 'pp', fwd_perm)]
    dot_general x160 -> x0, matrix products: 1870 us -> none  [the longest x64 645 us: cell_step(): jnp.dot(h_prev, w_hid, preferred_element_type=jnp.float32)]
    pallas_call x0 -> x3, Pallas kernels: none -> 1190 us  [the longest x1 666 us: local_fn(): pl.pallas_call(functools.partial(_bwd_kernel, n_stages, n_steps, n_blk, s...]
    ppermute x22 -> x0, starting transfers between devices: 926 us -> none  [the longest x11 823 us: bwd_tick(): inbox = lax.ppermute(jnp.stack(outbox), 'pp', bwd_perm)]
    concatenate x136 -> x0, other arithmetic: 448 us -> none  [the longest x128 393 us: cell_grad(): jnp.concatenate([dc_total * gate_g * gate_i * (1.0 - gate_i), dc_total *...]
    dynamic_update_slice x84 -> x0, local copies, waits for them, and re-layouts: 334 us -> none  [the longest x20 267 us: place(): return lax.dynamic_update_slice_in_dim(buf, piece, start, 0)]
    squeeze x82 -> x0, local copies, waits for them, and re-layouts: 280 us -> none  [the longest x64 155 us: seq_forward(): lax.scan(step_fn, (h_prev, c_prev), projected)]
    another operation x69 -> x0, other arithmetic: 265 us -> none  [the longest x25 160 us: bwd_tick(): inbox = lax.ppermute(jnp.stack(outbox), 'pp', bwd_perm)]
  transfers between devices with their start and end apart: 22 -> 0, of which waited for: 22 -> 0; matrix products, arithmetic and copies ran while one was open for 0% -> 0% of each run, Pallas kernels for 0% -> 0%
where the time goes in v1:
time: 1470 us
  Pallas kernels  1190 us (81%)
  local copies, waits for them, and re-layouts  267 us (18%)
    pallas_call x1, Pallas kernels, local_fn(): pl.pallas_call(functools.partial(_bwd_kernel, n_stages, n_steps, n_blk, s...  666 us
    pallas_call x1, Pallas kernels, local_fn(): pl.pallas_call(functools.partial(_fwd_kernel, n_stages, n_steps, n_blk),...  357 us
    pallas_call x1, Pallas kernels, local_fn(): pl.pallas_call(functools.partial(_dense_kernel, n_hid, n_blk, n_chunk), g...  171 us
    unnamed x14, local copies, waits for them, and re-layouts  95.2 us
    reshape x3, local copies, waits for them, and re-layouts, pack(): jnp.transpose(parts, (0, 3, 1, 2, 4))  55.5 us
    transpose x2, local copies, waits for them, and re-layouts, pack(): jnp.transpose(parts, (0, 3, 1, 2, 4))  52.6 us

profile of v1, /device:TPU:0, one launch (start us, length us, event | category | flops | bytes accessed | tf_op | source)
XLA Modules:
  0.0 1470.5 jit_solution(7769673274715789531)
XLA Ops:
  0.6 21.1 %copy.22 = bf16[2,1,1000,4000]{2,3,0,1:T(8,128)(2,1)} copy(bf16[2,1,1000,4000]{3,2,1,0:T(8,128)(2,1)} %param.9) | data formatting | bytes 32000000 | tf_op args[2]
  21.7 14.1 pad.27
  35.8 26.3 %copy.23 = bf16[2,4,1024,4,256]{4,3,2,1,0:T(4,128)(2,1)} copy(bf16[2,4,1024,4,256]{2,4,1,3,0:T(8,128)(2,1)} %bitcast.34) | data formatting | bytes 33554432 | tf_op jit(solution)/shard_map/transpose | solution.py:443
  62.1 27.4 %reshape.40.wx_hbm = bf16[2,4,1024,1024]{3,2,1,0:T(8,128)(2,1)} reshape(bf16[2,4,1024,4,256]{4,3,2,1,0:T(4,128)(2,1)} %copy.23) | data formatting | bytes 33554432 | tf_op jit(solution)/shard_map/reshape | solution.py:443
  89.5 21.1 %copy.24 = bf16[2,1,1000,4000]{2,3,0,1:T(8,128)(2,1)} copy(bf16[2,1,1000,4000]{3,2,1,0:T(8,128)(2,1)} %param.10) | data formatting | bytes 32000000 | tf_op args[3]
  110.6 14.1 pad.28
  124.7 26.3 %copy.25 = bf16[2,4,1024,4,256]{4,3,2,1,0:T(4,128)(2,1)} copy(bf16[2,4,1024,4,256]{2,4,1,3,0:T(8,128)(2,1)} %bitcast.35) | data formatting | bytes 33554432 | tf_op jit(solution)/shard_map/transpose | solution.py:443
  151.0 27.4 %reshape.42.wh_hbm = bf16[2,4,1024,1024]{3,2,1,0:T(8,128)(2,1)} reshape(bf16[2,4,1024,4,256]{4,3,2,1,0:T(4,128)(2,1)} %copy.25) | data formatting | bytes 33554432 | tf_op jit(solution)/shard_map/reshape | solution.py:443
  178.4 22.4 %copy.21 = bf16[256,32,1000]{2,0,1:T(8,128)(2,1)} copy(bf16[256,32,1000]{0,2,1:T(8,128)(2,1)} %param.7) | data formatting | bytes 32768000 | tf_op args[0]
  200.8 14.2 pad.26.seq0
  215.0 1.9 copy.27
  216.9 1.5 pad.31.c0
  218.4 1.7 copy.26
  220.1 1.1 pad.30.h0
  222.1 356.9 %lstm_forward.1 = (bf16[2,32,256,1024]{3,2,1,0:T(8,128)(2,1)}, bf16[2,32,1024,256]{3,2,1,0:T(8,128)(2,1)}, bf16[2,32,1024,256]{3,2,1,0:T(8,128)(2,1)}, f32[2,32,...) custom-call(bf16[32,256,1024]{2,1,0:T(8,128)(2,1)} %pad.26.seq0, ...), custom_call_target="tpu_custom_call" | custom-call | flops 274877906944 | tf_op jit(solution)/shard_map/lstm_forward/pallas_call | solution.py:460
  579.0 22.4 %copy.28 = bf16[256,32,1000]{2,0,1:T(8,128)(2,1)} copy(bf16[256,32,1000]{0,2,1:T(8,128)(2,1)} %param.8) | data formatting | bytes 32768000 | tf_op args[1]
  601.4 14.2 pad.32.target
  615.6 665.8 %lstm_backward.1 = (bf16[2,32,256,1024]{3,2,1,0:T(8,128)(2,1)}, bf16[2,32,4,256,1024]{4,3,2,1,0:T(8,128)(2,1)}, f32[2,4,1024,1024]{3,2,1,0:T(8,128)}, f32[2,4,8,...) custom-call(f32[2,32,4,256,1024]{4,3,2,1,0:T(8,128)} %get-tuple-element.19.gates, ...), custom_call_target="tpu_custom_call" | custom-call | flops 412316860416 | tf_op jit(solution)/shard_map/lstm_backward/pallas_call | solution.py:472
  1281.3 171.2 %input_weight_grad.1 = (f32[2,1000,4000]{2,1,0:T(8,128)}, f32[2,1000,4000]{2,1,0:T(8,128)}) custom-call(bf16[2,32,1024,256]{3,2,1,0:T(8,128)(2,1)} %get-tuple-element.24.r_ref, bf16[2,32,4,256,1024]{4,3,2,1,0:T(8,128)(2,1)} %get-tuple-element.25.z_ref, f32[2,4,1024,1024]{3,2,1,0:T(8,128)} %get-tuple-element.26.packed_ref), custom_call_target="tpu_custom_call" | custom-call | flops 137438953472 | tf_op jit(solution)/shard_map/input_weight_grad/pallas_call | solution.py:489
  1452.6 4.1 slice_bitcast_fusion
  1456.7 2.9 copy.31
  1459.5 1.8 copy.32
  1461.4 0.7 broadcast_in_dim_reshape.3
  1463.4 6.9 psum.7
  (13 shorter events, 1.6 us)
Async XLA Ops:
  200.8 20.4 %copy-start.1 = (f32[2,1,4000]{2,1,0:T(1,128)S(1)}, f32[2,1,4000]{2,1,0:T(1,128)}, u32[]{:S(2)}) copy-start(f32[2,1,4000]{2,1,0:T(1,128)} %param.11) | copy-start | bytes 96004
  1452.6 8.7 copy-start
  1452.6 9.6 copy-start.2

commit v2 on v0

v2 whole, which is shorter than its diff:
```python
import functools

import jax
import jax.numpy as jnp
from jax import lax
from jax.experimental import pallas as pl
from jax.experimental.pallas import tpu as pltpu
from jax.sharding import PartitionSpec as P

F32 = jnp.float32
BF16 = jnp.bfloat16
MESH = pl.DeviceIdType.MESH
LANES = 128
BLK = 256
FINE = 128
ROWS = 16
SLOTS = 4
VMEM_LIMIT = 67043328
ALONG_LANES = (((1,), (1,)), ((), ()))


def _blocks(n_hid, block=BLK):
    return [(r, min(block, n_hid - r)) for r in range(0, n_hid, block)]


def _chunks(first, count):
    return [(first + r, min(ROWS, count - r)) for r in range(0, count, ROWS)]


def _segments(n_hid, first, count):
    runs, n = [], first
    while n < first + count:
        gate, hid = n // n_hid, n % n_hid
        base = hid // FINE * FINE
        size = min(FINE, n_hid - base)
        length = min(first + count - n, base + size - hid)
        runs.append((n - first, length, 4 * base + gate * size + hid - base, gate))
        n += length
    return runs


def _enter(n_stages):
    stage = lax.axis_index('pp')
    nxt = lax.rem(stage + 1, n_stages)
    prv = lax.rem(stage + n_stages - 1, n_stages)
    barrier = pltpu.get_barrier_semaphore()
    for peer in (nxt, prv):
        pl.semaphore_signal(barrier, inc=1, device_id={'pp': peer}, device_id_type=MESH)
    pl.semaphore_wait(barrier, 2)
    return stage, nxt, prv


def _fwd_kernel(n_stages, n_steps, n_hid, seq0, wx_hbm, wh_hbm, bias_in, h0, c0, wrap, r_seq, h_seq, saved, top, wt, stage_buf, eye, bias, ring, hb0, hb1, cell, zb0, zb1, fb0, fb1, ob, w_sem, x_sem, r_sem, f_sem, h_sem, o_sem, i_sem, recv_sem, wrap_sem, free_sem):
    n_total = 2 * n_steps
    n_gate = 4 * n_hid
    n_pad = wt.shape[-1]
    blocks = _blocks(n_hid, FINE)
    parts = _blocks(n_hid)
    hb, fb, zb = (hb0, hb1), (fb0, fb1), (zb0, zb1)
    valid = pl.ds(0, n_hid)
    n_cut = n_pad // BLK
    tail = n_hid - (n_cut - 1) * BLK
    halved = (0.5, 0.5, 1.0, 0.5)

    def unit_copies(k, m, act):
        mat, cut = m // n_cut, lax.rem(m, n_cut)
        slot = lax.rem(m, 2)
        for which, src in enumerate((wx_hbm, wh_hbm)):

            @pl.when((mat == which) & (cut < n_cut - 1))
            def _(src=src):
                act(pltpu.make_async_copy(src.at[k, pl.ds(pl.multiple_of(cut * BLK, BLK), BLK)], stage_buf.at[slot], w_sem.at[slot]))

            @pl.when((mat == which) & (cut == n_cut - 1))
            def _(src=src):
                act(pltpu.make_async_copy(src.at[k, pl.ds((n_cut - 1) * BLK, tail)], stage_buf.at[slot, pl.ds(0, tail)], w_sem.at[slot]))

    def transpose_unit(k, m):
        mat, cut = m // n_cut, lax.rem(m, n_cut)
        slot = lax.rem(m, 2)
        unit_copies(k, m, lambda copy: copy.wait())

        @pl.when(cut == n_cut - 1)
        def _():
            stage_buf[slot, tail:, :] = jnp.zeros((BLK - tail, n_gate), BF16)

        for n in range(0, n_gate, BLK):
            width = min(BLK, n_gate - n)
            tile = lax.dot_general(eye[0:width, 0:width], stage_buf[slot, :, n:n + width], ALONG_LANES, preferred_element_type=F32)
            for at, length, row, gate in _segments(n_hid, n, width):
                wt[mat, k, pl.ds(row, length), pl.ds(pl.multiple_of(cut * BLK, BLK), BLK)] = (tile[at:at + length] * halved[gate]).astype(BF16)

        @pl.when(m + 2 < 2 * n_cut)
        def _():
            unit_copies(k, m + 2, lambda copy: copy.start())

    def spread_bias(k):
        for n in range(0, n_gate, LANES):
            width = min(LANES, n_gate - n)
            tile = jnp.broadcast_to(bias_in[k, :, n:n + width], (LANES, width)).T
            for at, length, row, gate in _segments(n_hid, n, width):
                bias[row:row + length, :] = tile[at:at + length] * halved[gate]

    unit_copies(0, 0, lambda copy: copy.start())
    unit_copies(0, 1, lambda copy: copy.start())
    for buf in (hb0, hb1):
        buf[n_hid:, :] = jnp.zeros((n_pad - n_hid, buf.shape[1]), BF16)
    for s in range(SLOTS):
        ring[s, n_hid:, :] = jnp.zeros((n_pad - n_hid, ring.shape[2]), BF16)
    eye[...] = (lax.broadcasted_iota(jnp.int32, (BLK, BLK), 0) == lax.broadcasted_iota(jnp.int32, (BLK, BLK), 1)).astype(F32).astype(BF16)
    stage, nxt, prv = _enter(n_stages)
    is_first = stage == 0
    is_last = stage == n_stages - 1

    def fetch(n):
        k, t = n // n_steps, lax.rem(n, n_steps)
        slot = lax.rem(n, SLOTS)

        @pl.when(is_first & (k == 0))
        def _():
            pltpu.make_async_copy(seq0.at[t], ring.at[slot, valid], x_sem.at[slot]).start()

        @pl.when(is_first & (k == 1))
        def _():
            pltpu.make_async_remote_copy(src_ref=ob.at[0], dst_ref=wrap.at[t], send_sem=o_sem.at[0, 0], recv_sem=wrap_sem.at[t], device_id={'pp': nxt}, device_id_type=MESH).wait_recv()
            pltpu.make_async_copy(wrap.at[t], ring.at[slot, valid], x_sem.at[slot]).start()

    def arrive(n):
        slot = lax.rem(n, SLOTS)

        @pl.when(is_first)
        def _():
            pltpu.make_async_copy(seq0.at[0], ring.at[slot, valid], x_sem.at[slot]).wait()

        @pl.when(jnp.logical_not(is_first))
        def _():
            pltpu.make_async_remote_copy(src_ref=ob.at[0], dst_ref=ring.at[slot, valid], send_sem=o_sem.at[0, 0], recv_sem=recv_sem.at[slot], device_id={'pp': nxt}, device_id_type=MESH).wait_recv()

    def store_x(n):
        slot = lax.rem(n, SLOTS)
        return pltpu.make_async_copy(ring.at[slot, valid], r_seq.at[n // n_steps, lax.rem(n, n_steps)], r_sem.at[slot])

    def outgoing(n, j, act):
        k, t = n // n_steps, lax.rem(n, n_steps)
        slot = lax.rem(n, SLOTS)
        rows = pl.ds(*parts[j])

        @pl.when(jnp.logical_not(is_last))
        def _():
            act(pltpu.make_async_remote_copy(src_ref=ob.at[slot, rows], dst_ref=ring.at[slot, rows], send_sem=o_sem.at[slot, j], recv_sem=recv_sem.at[slot], device_id={'pp': nxt}, device_id_type=MESH), True)

        @pl.when(is_last & (k == 0))
        def _():
            act(pltpu.make_async_remote_copy(src_ref=ob.at[slot, rows], dst_ref=wrap.at[t, rows], send_sem=o_sem.at[slot, j], recv_sem=wrap_sem.at[t], device_id={'pp': nxt}, device_id_type=MESH), True)

        @pl.when(is_last & (k == 1))
        def _():
            act(pltpu.make_async_copy(ob.at[slot, rows], top.at[t, rows], o_sem.at[slot, j]), False)

    def start(copy, remote):
        copy.start()

    def finish(copy, remote):
        if remote:
            copy.wait_send()
        else:
            copy.wait()

    def h_copy(n, u):
        return pltpu.make_async_copy(hb[u].at[valid], h_seq.at[n // n_steps, lax.rem(n, n_steps) + 1], h_sem.at[u])

    def f_copy(n, u):
        return pltpu.make_async_copy(fb[u], saved.at[n // n_steps, lax.rem(n, n_steps)], f_sem.at[u])

    fetch(0)

    def build(m, carry):
        transpose_unit(0, m)
        return carry

    lax.fori_loop(0, 2 * n_cut, build, 0)
    unit_copies(1, 0, lambda copy: copy.start())
    unit_copies(1, 1, lambda copy: copy.start())

    def step(n, u):
        k, t = n // n_steps, lax.rem(n, n_steps)
        slot = lax.rem(n, SLOTS)
        v = 1 - u

        @pl.when((n >= 2) & (n != n_steps + 1))
        def _():
            f_copy(n - 2, u).wait()

        @pl.when(n >= SLOTS)
        def _():
            for j in range(len(parts)):
                outgoing(n - SLOTS, j, finish)

        @pl.when(n >= 2 - u)
        def _():
            h_copy(0, u).wait()

        if u == 0:

            @pl.when(t == 0)
            def _():
                h_in = pltpu.make_async_copy(h0.at[k], fb[v].at[5], i_sem.at[0])
                c_in = pltpu.make_async_copy(c0.at[k], cell, i_sem.at[1])
                @pl.when(n > 0)
                def _():
                    h_copy(n - 1, v).wait()
                    f_copy(n - 1, v).wait()

                h_in.start()
                c_in.start()

                spread_bias(k)
                h_in.wait()
                c_in.wait()
                hb[v][0:n_hid, :] = fb[v][5, :, :].astype(BF16)
                pltpu.make_async_copy(hb[v].at[valid], h_seq.at[k, 0], h_sem.at[v]).start()

            every = n_steps // (2 * n_cut)

            @pl.when((n < n_steps) & (lax.rem(n, every) == 0))
            def _():
                transpose_unit(1, n // every)

        arrive(n)
        store_x(n).start()

        @pl.when(n + 1 < n_total)
        def _():
            fetch(n + 1)

        for j, (first, size) in enumerate(blocks):
            gate_rows = pl.ds(4 * first, 4 * size)
            z = zb[j % len(zb)]
            z[0:4 * size, :] = jnp.dot(wt[0, k, gate_rows, :], ring[slot], preferred_element_type=F32) + jnp.dot(wt[1, k, gate_rows, :], hb[v][...], preferred_element_type=F32)
            for r, count in _chunks(first, size):
                rows = pl.ds(r, count)
                pre = []
                for g in range(4):
                    at = g * size + r - first
                    pre.append(z[at:at + count, :] + jnp.concatenate([bias[4 * first + at:4 * first + at + count, :]] * 2, axis=1))
                gate_i = 0.5 * jnp.tanh(pre[0]) + 0.5
                gate_f = 0.5 * jnp.tanh(pre[1]) + 0.5
                gate_g = jnp.tanh(pre[2])
                gate_o = 0.5 * jnp.tanh(pre[3]) + 0.5
                c_old = cell[rows, :]
                c_new = gate_f * c_old + gate_i * gate_g
                tanh_c = jnp.tanh(c_new)
                h_wide = gate_o * tanh_c
                h_new = h_wide.astype(BF16)
                cell[rows, :] = c_new
                hb[u][rows, :] = h_new
                ob[slot, rows, :] = (ring[slot, rows, :].astype(F32) + h_new.astype(F32)).astype(BF16)
                fb[u][0, rows, :] = gate_i * gate_g * (1.0 - gate_i)
                fb[u][1, rows, :] = gate_f * c_old * (1.0 - gate_f)
                fb[u][2, rows, :] = gate_i * (1.0 - gate_g * gate_g)
                fb[u][3, rows, :] = h_wide * (1.0 - gate_o)
                fb[u][4, rows, :] = gate_o * (1.0 - tanh_c * tanh_c)
                fb[u][5, rows, :] = gate_f

        @pl.when(jnp.logical_not(is_last) & (n >= SLOTS))
        def _():
            pl.semaphore_wait(free_sem, 1)

        for j in range(len(parts)):
            outgoing(n, j, start)
        f_copy(n, u).start()
        h_copy(n, u).start()

        @pl.when(n >= 1)
        def _():
            store_x(n - 1).wait()

        @pl.when(jnp.logical_not(is_first) & (n >= 1) & (n <= n_total - SLOTS))
        def _():
            pl.semaphore_signal(free_sem, inc=1, device_id={'pp': prv}, device_id_type=MESH)

    def pair(i, carry):
        step(2 * i, 0)
        step(2 * i + 1, 1)
        return carry

    lax.fori_loop(0, n_steps, pair, 0)
    store_x(n_total - 1).wait()
    for n in range(n_total - SLOTS, n_total):
        for j in range(len(parts)):
            outgoing(n, j, finish)
    for n, u in ((n_total - 2, 0), (n_total - 1, 1)):
        f_copy(n, u).wait()
        h_copy(n, u).wait()


def _bwd_kernel(n_stages, n_steps, n_hid, scale, saved, h_seq, top, target, wx_hbm, wh_hbm, wrap, dz_seq, dwh, db, dh_out, dc_out, loss, wx, wh, acc, zb0, zb1, fb0, fb1, ring, tb0, tb1, ob0, ob1, hb0, hb1, dh, dc, gin, bacc, lacc, lbuf, w_sem, s_sem, a_sem, t_sem, h_sem, z_sem, o_sem, f_sem, recv_sem, wrap_sem, l_sem, free_sem):
    n_total = 2 * n_steps
    n_gate = 4 * n_hid
    blocks = _blocks(n_hid)
    valid = pl.ds(0, n_hid)
    n_tiles = [(n, min(4 * BLK, n_gate - n)) for n in range(0, n_gate, 4 * BLK)]
    zb, fb, tb, ob, hb = (zb0, zb1), (fb0, fb1), (tb0, tb1), (ob0, ob1), (hb0, hb1)

    def weight_copies(k):
        return [pltpu.make_async_copy(wh_hbm.at[k], wh, w_sem.at[0]), pltpu.make_async_copy(wx_hbm.at[k], wx, w_sem.at[1])]

    def place(n):
        return 1 - n // n_steps, n_steps - 1 - lax.rem(n, n_steps)

    def fetch_saved(n, u):
        k, t = place(n)
        pltpu.make_async_copy(saved.at[k, t], fb[u], s_sem.at[u]).start()

    def wait_saved(u):
        pltpu.make_async_copy(saved.at[0, 0], fb[u], s_sem.at[u]).wait()

    def fetch_h(n, u):
        k, t = place(n)
        pltpu.make_async_copy(h_seq.at[k, t], hb[u].at[valid], h_sem.at[u]).start()

    def wait_h(u):
        pltpu.make_async_copy(h_seq.at[0, 0], hb[u].at[valid], h_sem.at[u]).wait()

    for copy in weight_copies(1):
        copy.start()
    fetch_saved(0, 0)
    acc[...] = jnp.zeros_like(acc)
    for buf in (dh, dc, tb0, tb1, zb1, hb0, hb1, lacc, bacc):
        buf[...] = jnp.zeros_like(buf)
    stage, nxt, prv = _enter(n_stages)
    is_first = stage == 0
    is_last = stage == n_stages - 1

    def fetch_grad(n, u):
        k, t = place(n)
        slot = lax.rem(n, SLOTS)

        @pl.when(is_last & (k == 1))
        def _():
            pltpu.make_async_copy(top.at[t], ring.at[slot], a_sem.at[slot]).start()
            pltpu.make_async_copy(target.at[t], tb[u], t_sem.at[u]).start()

        @pl.when(is_last & (k == 0))
        def _():
            pltpu.make_async_remote_copy(src_ref=ob0, dst_ref=wrap.at[t], send_sem=o_sem.at[0, 0], recv_sem=wrap_sem.at[t], device_id={'pp': prv}, device_id_type=MESH).wait_recv()
            pltpu.make_async_copy(wrap.at[t], ring.at[slot], a_sem.at[slot]).start()

    def wait_grad(n, u):
        slot = lax.rem(n, SLOTS)

        @pl.when(is_last)
        def _():
            pltpu.make_async_copy(top.at[0], ring.at[slot], a_sem.at[slot]).wait()

        @pl.when(is_last & (n < n_steps))
        def _():
            pltpu.make_async_copy(target.at[0], tb[u], t_sem.at[u]).wait()

        @pl.when(jnp.logical_not(is_last))
        def _():
            pltpu.make_async_remote_copy(src_ref=ob0, dst_ref=ring.at[slot], send_sem=o_sem.at[0, 0], recv_sem=recv_sem.at[slot], device_id={'pp': prv}, device_id_type=MESH).wait_recv()

    def outgoing(n, u, j, act):
        k, t = place(n)
        slot = lax.rem(n, SLOTS)
        rows = pl.ds(*blocks[j])

        @pl.when(jnp.logical_not(is_first))
        def _():
            act(pltpu.make_async_remote_copy(src_ref=ob[u].at[rows], dst_ref=ring.at[slot, rows], send_sem=o_sem.at[u, j], recv_sem=recv_sem.at[slot], device_id={'pp': prv}, device_id_type=MESH))

        @pl.when(is_first & (k == 1))
        def _():
            act(pltpu.make_async_remote_copy(src_ref=ob[u].at[rows], dst_ref=wrap.at[t, rows], send_sem=o_sem.at[u, j], recv_sem=wrap_sem.at[t], device_id={'pp': prv}, device_id_type=MESH))

    def dz_copy(n, u):
        k, t = place(n)
        return pltpu.make_async_copy(zb[u], dz_seq.at[k, t], z_sem.at[u])

    def weight_grad(v, i):
        n, m = n_tiles[i]
        acc[:, n:n + m] += lax.dot_general(hb[v][...], zb[v][n:n + m, :], ALONG_LANES, preferred_element_type=F32)

    def acc_copy(k):
        return pltpu.make_async_copy(acc.at[valid], dwh.at[k], f_sem.at[0])

    def state_copies(k):
        return [pltpu.make_async_copy(dh, dh_out.at[k], f_sem.at[1]), pltpu.make_async_copy(dc, dc_out.at[k], f_sem.at[2])]

    fetch_h(0, 0)

    def relay():
        return pltpu.make_async_remote_copy(src_ref=lbuf, dst_ref=lbuf, send_sem=l_sem.at[0], recv_sem=l_sem.at[1], device_id={'pp': prv}, device_id_type=MESH)

    fetch_grad(0, 0)
    for copy in weight_copies(1):
        copy.wait()

    def step(n, u):
        k, t = place(n)
        slot = lax.rem(n, SLOTS)
        v = 1 - u
        if u == 0:

            @pl.when(n == n_steps)
            def _():
                for copy in weight_copies(0) + state_copies(1):
                    copy.start()
                for copy in state_copies(1):
                    copy.wait()
                for buf in (dh, dc, tb0, tb1):
                    buf[...] = jnp.zeros_like(buf)
                for copy in weight_copies(0):
                    copy.wait()

        else:

            @pl.when(n == n_steps + 1)
            def _():
                acc_copy(1).wait()
                acc[...] = jnp.zeros_like(acc)

        @pl.when(n >= 2)
        def _():
            dz_copy(n - 2, u).wait()
            for j in range(len(blocks)):
                outgoing(n - 2, u, j, lambda copy: copy.wait_send())

        if u == 0:

            @pl.when(n > 0)
            def _():
                wait_h(v)
        else:
            wait_h(v)
        wait_saved(u)
        wait_grad(n, u)

        @pl.when(n + 1 < n_total)
        def _():
            fetch_saved(n + 1, v)
            fetch_grad(n + 1, v)

        mult = jnp.where(is_last & (k == 1), scale, 1.0).astype(F32)
        for i, (first, size) in enumerate(blocks):
            weight_grad(v, i)
            square = jnp.zeros((8, BLK), F32)
            for r, count in _chunks(first, size):
                rows = pl.ds(r, count)
                diff = ring[slot, rows, :].astype(F32) - tb[u][rows, :].astype(F32)
                for e in range(0, count, 8):
                    square = square + diff[e:e + 8] * diff[e:e + 8]
                into = diff * mult
                gin[rows, :] = into
                dh_all = into + dh[rows, :]
                dc_all = dc[rows, :] + dh_all * fb[u][4, rows, :]
                dc[rows, :] = dc_all * fb[u][5, rows, :]
                for g in range(4):
                    dz = (dh_all if g == 3 else dc_all) * fb[u][g, rows, :]
                    at = pl.ds(g * n_hid + r, count)
                    bacc[k, at, :] += dz[:, :LANES] + dz[:, LANES:]
                    zb[u][at, :] = dz.astype(BF16)
            lacc[...] += square
            if i + 1 < len(blocks):
                hb[v][n_hid:, :] = zb[u][first + size - 8:first + size, :]
        for first, size in blocks:
            dh[pl.ds(first, size), :] = jnp.dot(wh[pl.ds(first, size), :], zb[u][...], preferred_element_type=F32)
        for first, size in blocks:
            rows = pl.ds(first, size)
            ob[u][rows, :] = (gin[rows, :] + jnp.dot(wx[rows, :], zb[u][...], preferred_element_type=F32)).astype(BF16)

        @pl.when(jnp.logical_not(is_first) & (n >= SLOTS))
        def _():
            pl.semaphore_wait(free_sem, 1)

        for j in range(len(blocks)):
            outgoing(n, u, j, lambda copy: copy.start())
        dz_copy(n, u).start()

        @pl.when(jnp.logical_not(is_last) & (n < n_total - SLOTS))
        def _():
            pl.semaphore_signal(free_sem, inc=1, device_id={'pp': nxt}, device_id_type=MESH)

        @pl.when(n + 1 < n_total)
        def _():
            fetch_h(n + 1, v)

        if u == 0:

            @pl.when(n == n_steps)
            def _():
                acc_copy(1).start()

        else:

            @pl.when(is_last & (n == n_steps - 1))
            def _():
                lbuf[...] = lacc[...]
                relay().start()

            @pl.when(jnp.logical_not(is_last) & (n == n_steps + 1))
            def _():
                relay().wait_recv()

                @pl.when(jnp.logical_not(is_first))
                def _():
                    relay().start()

    def pair(i, carry):
        step(2 * i, 0)
        step(2 * i + 1, 1)
        return carry

    lax.fori_loop(0, n_steps, pair, 0)
    wait_h(1)
    last = []
    for i, (n, m) in enumerate(n_tiles):
        weight_grad(1, i)
        last.append(pltpu.make_async_copy(acc.at[valid, pl.ds(n, m)], dwh.at[0, :, pl.ds(n, m)], w_sem.at[i]))
        last[-1].start()
    flush = [pltpu.make_async_copy(bacc, db, f_sem.at[3]), pltpu.make_async_copy(lbuf, loss, f_sem.at[4])] + state_copies(0)
    for copy in flush:
        copy.start()
    for n, u in ((n_total - 2, 0), (n_total - 1, 1)):
        dz_copy(n, u).wait()
        for j in range(len(blocks)):
            outgoing(n, u, j, lambda copy: copy.wait_send())

    @pl.when(jnp.logical_not(is_first))
    def _():
        relay().wait_send()

    for copy in last + flush:
        copy.wait()


def _dense_kernel(n_chunk, half, r_ref, z_ref, dwh_in, db_in, dh_in, dc_in, loss_in, dwx_ref, dwh_ref, db_ref, dh_ref, dc_ref, loss_ref):
    @pl.when(pl.program_id(2) == 0)
    def _():
        dwx_ref[...] = jnp.zeros_like(dwx_ref)
        loss_ref[...] = half * jnp.sum(jnp.sum(loss_in[...], axis=0, keepdims=True), axis=1, keepdims=True)

    n_gate = dwx_ref.shape[-1]
    for n in range(0, n_gate, 4 * BLK):
        m = min(4 * BLK, n_gate - n)
        dwx_ref[0, :, n:n + m] += sum(lax.dot_general(r_ref[0, t], z_ref[0, t, n:n + m, :], ALONG_LANES, preferred_element_type=F32) for t in range(n_chunk))
    dwh_ref[...] = dwh_in[...]
    dh_ref[...] = dh_in[...]
    dc_ref[...] = dc_in[...]
    for n in range(0, db_in.shape[1], LANES):
        db_ref[0, :, n:n + LANES] = jnp.sum(db_in[0, n:n + LANES, :].T, axis=0, keepdims=True)


def solution(mesh):
    n_stages = mesh.shape['pp']

    def local_fn(inputs, targets, w_in, w_hid, bias, h_init, c_init):
        n_batch, n_steps, n_hid = inputs.shape
        n_gate = 4 * n_hid
        n_pad = -(-n_hid // BLK) * BLK
        n_blk = len(_blocks(n_hid))
        seq0 = jnp.transpose(inputs, (1, 2, 0))
        target = jnp.transpose(targets, (1, 2, 0))
        h0 = jnp.transpose(h_init[:, 0], (0, 2, 1))
        c0 = jnp.transpose(c_init[:, 0], (0, 2, 1))
        wx, wh = w_in[:, 0], w_hid[:, 0]

        def shape(*dims, dtype=BF16):
            return jax.ShapeDtypeStruct(dims, dtype)

        any_spec = pl.BlockSpec(memory_space=pl.ANY)
        vmem_spec = pl.BlockSpec(memory_space=pltpu.VMEM)
        row = (n_hid, n_batch)
        wide = (n_pad, n_batch)
        tall = (n_gate, n_batch)
        dma = pltpu.SemaphoreType.DMA
        step_flops = 2 * n_batch * n_hid * n_gate
        _, r_seq, h_seq, saved, top = pl.pallas_call(
            functools.partial(_fwd_kernel, n_stages, n_steps, n_hid),
            out_shape=(shape(n_steps, *row), shape(2, n_steps, *row), shape(2, n_steps + 1, *row), shape(2, n_steps, 6, *row, dtype=F32), shape(n_steps, *row)),
            in_specs=[any_spec, any_spec, any_spec, vmem_spec, any_spec, any_spec],
            out_specs=[any_spec] * 5,
            scratch_shapes=[pltpu.VMEM((2, 2, n_gate, n_pad), BF16), pltpu.VMEM((2, BLK, n_gate), BF16), pltpu.VMEM((BLK, BLK), BF16), pltpu.VMEM((n_gate, LANES), F32), pltpu.VMEM((SLOTS, *wide), BF16)] + [pltpu.VMEM(wide, BF16)] * 2 + [pltpu.VMEM(row, F32)] + [pltpu.VMEM((4 * FINE, n_batch), F32)] * 2 + [pltpu.VMEM((6, *row), F32)] * 2 + [pltpu.VMEM((SLOTS, *row), BF16)] + [dma((2,)), dma((SLOTS,)), dma((SLOTS,)), dma((2,)), dma((2,)), dma((SLOTS, n_blk)), dma((2,)), dma((SLOTS,)), dma((n_steps,)), pltpu.SemaphoreType.REGULAR],
            compiler_params=pltpu.CompilerParams(collective_id=0, has_side_effects=True, vmem_limit_bytes=VMEM_LIMIT),
            cost_estimate=pl.CostEstimate(flops=4 * n_steps * step_flops, bytes_accessed=0, transcendentals=0),
            name='lstm_forward',
        )(seq0, wx, wh, bias, h0, c0)

        scale = 1.0 / (n_batch * n_steps)
        _, dz_seq, dwh_p, db_p, dh_p, dc_p, loss_p = pl.pallas_call(
            functools.partial(_bwd_kernel, n_stages, n_steps, n_hid, scale),
            out_shape=(shape(n_steps, *row), shape(2, n_steps, *tall), shape(2, n_hid, n_gate, dtype=F32), shape(2, n_gate, LANES, dtype=F32), shape(2, *row, dtype=F32), shape(2, *row, dtype=F32), shape(8, n_batch, dtype=F32)),
            in_specs=[any_spec] * 6,
            out_specs=[any_spec] * 7,
            scratch_shapes=[pltpu.VMEM((n_hid, n_gate), BF16)] * 2 + [pltpu.VMEM((n_hid + 8, n_gate), F32)] + [pltpu.VMEM(tall, BF16)] * 2 + [pltpu.VMEM((6, *row), F32)] * 2 + [pltpu.VMEM((SLOTS, *row), BF16)] + [pltpu.VMEM(row, BF16)] * 4 + [pltpu.VMEM((n_hid + 8, n_batch), BF16)] * 2 + [pltpu.VMEM(row, F32)] * 3 + [pltpu.VMEM((2, n_gate, LANES), F32)] + [pltpu.VMEM((8, n_batch), F32)] * 2 + [dma((n_blk,)), dma((2,)), dma((SLOTS,)), dma((2,)), dma((2,)), dma((2,)), dma((2, n_blk)), dma((5,)), dma((SLOTS,)), dma((n_steps,)), dma((2,)), pltpu.SemaphoreType.REGULAR],
            compiler_params=pltpu.CompilerParams(collective_id=1, has_side_effects=True, vmem_limit_bytes=VMEM_LIMIT),
            cost_estimate=pl.CostEstimate(flops=6 * n_steps * step_flops, bytes_accessed=0, transcendentals=0),
            name='lstm_backward',
        )(saved, h_seq, top, target, wx, wh)

        n_chunk = 4
        n_part = 2 * n_steps // n_chunk
        p_rows = n_pad // n_part
        half_gate = n_blk * BLK * 2
        part = lambda k, h, c: (k, h * (n_steps // n_chunk) + c, 0)
        dwx, dwh, db, dh, dc, loss = pl.pallas_call(
            functools.partial(_dense_kernel, n_chunk, 0.5 * scale),
            grid=(2, 2, n_steps // n_chunk),
            out_shape=(shape(2, n_hid, n_gate, dtype=F32), shape(2, n_hid, n_gate, dtype=F32), shape(2, 1, n_gate, dtype=F32), shape(2, *row, dtype=F32), shape(2, *row, dtype=F32), shape(1, 1, dtype=F32)),
            in_specs=[pl.BlockSpec((1, n_chunk, *row), lambda k, h, c: (k, c, 0, 0)), pl.BlockSpec((1, n_chunk, half_gate, n_batch), lambda k, h, c: (k, c, h, 0)), pl.BlockSpec((1, p_rows, n_gate), part), pl.BlockSpec((1, 4 * p_rows, LANES), part), pl.BlockSpec((1, p_rows, n_batch), part), pl.BlockSpec((1, p_rows, n_batch), part), pl.BlockSpec((8, n_batch), lambda k, h, c: (0, 0))],
            out_specs=[pl.BlockSpec((1, n_hid, half_gate), lambda k, h, c: (k, 0, h)), pl.BlockSpec((1, p_rows, n_gate), part), pl.BlockSpec((1, 1, 4 * p_rows), lambda k, h, c: (k, 0, h * (n_steps // n_chunk) + c)), pl.BlockSpec((1, p_rows, n_batch), part), pl.BlockSpec((1, p_rows, n_batch), part), pl.BlockSpec((1, 1), lambda k, h, c: (0, 0))],
            compiler_params=pltpu.CompilerParams(dimension_semantics=('arbitrary', 'arbitrary', 'arbitrary'), vmem_limit_bytes=VMEM_LIMIT),
            cost_estimate=pl.CostEstimate(flops=2 * n_steps * step_flops, bytes_accessed=0, transcendentals=0),
            name='input_weight_grad',
        )(r_seq, dz_seq, dwh_p, db_p, dh_p, dc_p, loss_p)

        back = lambda g: jnp.transpose(g, (0, 2, 1))[:, None]
        return loss[0], dwx[:, None], dwh[:, None], db, back(dh), back(dc)

    spec_seq = P('dp', None, None)
    spec_weight = P('dp', 'pp', None, None)
    spec_bias = P('dp', 'pp', None)
    return jax.shard_map(local_fn, mesh=mesh, in_specs=(spec_seq, spec_seq, spec_weight, spec_weight, spec_bias, spec_weight, spec_weight), out_specs=(P('dp'), spec_weight, spec_weight, spec_bias, spec_weight, spec_weight), check_vma=False)
```

time: 7910 us -> 1070 us (0.14)
  waiting for transfers between devices: 2410 us -> 0 us
  matrix products: 1870 us -> 0 us
  other arithmetic: 1370 us -> 0 us
  local copies, waits for them, and re-layouts: 1200 us -> 0 us
  Pallas kernels: 0 us -> 1070 us
  starting transfers between devices: 926 us -> 0 us
  loops' own time: 107 us -> 0 us
    ppermute x22 -> x0, waiting for transfers between devices: 2410 us -> none  [the longest x11 1430 us: fwd_tick(): inbox = lax.ppermute(jnp.stack(outbox), 'pp', fwd_perm)]
    dot_general x160 -> x0, matrix products: 1870 us -> none  [the longest x64 645 us: cell_step(): jnp.dot(h_prev, w_hid, preferred_element_type=jnp.float32)]
    pallas_call x0 -> x3, Pallas kernels: none -> 1070 us  [the longest x1 552 us: local_fn(): pl.pallas_call(functools.partial(_bwd_kernel, n_stages, n_steps, n_hid, s...]
    ppermute x22 -> x0, starting transfers between devices: 926 us -> none  [the longest x11 823 us: bwd_tick(): inbox = lax.ppermute(jnp.stack(outbox), 'pp', bwd_perm)]
    concatenate x136 -> x0, other arithmetic: 448 us -> none  [the longest x128 393 us: cell_grad(): jnp.concatenate([dc_total * gate_g * gate_i * (1.0 - gate_i), dc_total *...]
    dynamic_update_slice x84 -> x0, local copies, waits for them, and re-layouts: 334 us -> none  [the longest x20 267 us: place(): return lax.dynamic_update_slice_in_dim(buf, piece, start, 0)]
    squeeze x82 -> x0, local copies, waits for them, and re-layouts: 280 us -> none  [the longest x64 155 us: seq_forward(): lax.scan(step_fn, (h_prev, c_prev), projected)]
    another operation x69 -> x0, other arithmetic: 265 us -> none  [the longest x25 160 us: bwd_tick(): inbox = lax.ppermute(jnp.stack(outbox), 'pp', bwd_perm)]
  transfers between devices with their start and end apart: 22 -> 0, of which waited for: 22 -> 0; matrix products, arithmetic and copies ran while one was open for 0% -> 0% of each run, Pallas kernels for 0% -> 0%
where the time goes in v2:
time: 1070 us
  Pallas kernels  1070 us (100%)
    pallas_call x1, Pallas kernels, local_fn(): pl.pallas_call(functools.partial(_bwd_kernel, n_stages, n_steps, n_hid, s...  552 us
    pallas_call x1, Pallas kernels, local_fn(): pl.pallas_call(functools.partial(_fwd_kernel, n_stages, n_steps, n_hid),...  357 us
    pallas_call x1, Pallas kernels, local_fn(): pl.pallas_call(functools.partial(_dense_kernel, n_chunk, 0.5 * scale), gr...  164 us

profile of v2, /device:TPU:0, one launch (start us, length us, event | category | flops | bytes accessed | tf_op | source)
XLA Modules:
  0.0 1073.1 jit_solution(3055133819701022638)
XLA Ops:
  0.6 357.1 %lstm_forward.1 = (bf16[32,1000,256]{2,1,0:T(8,128)(2,1)}, bf16[2,32,1000,256]{3,2,1,0:T(8,128)(2,1)}, bf16[2,33,1000,256]{3,2,1,0:T(8,128)(2,1)}, f32[2,32,6,10...) custom-call(bf16[32,1000,256]{2,1,0:T(8,128)(2,1)} %bitcast.27, bf16[2,1000,4000]{2,1,0:T(8,128)(2,1)} %bitcast.28, ...), custom_call_target="tpu_custom_call" | custom-call | flops 262144000000 | tf_op jit(solution)/shard_map/lstm_forward/pallas_call | solution.py:579
  357.7 551.7 %lstm_backward.1 = (bf16[32,1000,256]{2,1,0:T(8,128)(2,1)}, bf16[2,32,4000,256]{3,2,1,0:T(8,128)(2,1)}, f32[2,1000,4000]{2,1,0:T(8,128)}, f32[2,4000,128]{2,1,0:...) custom-call(f32[2,32,6,1000,256]{4,3,2,1,0:T(8,128)} %get-tuple-element.23.saved, ...), custom_call_target="tpu_custom_call" | custom-call | flops 393216000000 | tf_op jit(solution)/shard_map/lstm_backward/pallas_call | solution.py:591
  909.4 163.5 %input_weight_grad.1 = (f32[2,1000,4000]{2,1,0:T(8,128)}, f32[2,1000,4000]{2,1,0:T(8,128)}, f32[2,1,4000]{2,1,0:T(1,128)}, f32[2,1000,256]{2,1,0:T(8,128)}, f32[2,1000,256]{2,1,0:T(8,128)}, /*index=5*/f32[1,1]{1,0:T(1,128)}) custom-call(bf16[2,32,1000,256]{3,2,1,0:T(8,128)(2,1)} %get-tuple-element.22.r_ref, ...), custom_call_target="tpu_custom_call" | custom-call | flops 131072000000 | tf_op jit(solution)/shard_map/input_weight_grad/pallas_call | solution.py:607
